TPU v7x, 32 devices: a whole 2x2x4 slice. The times are simulated.
32 devices in a mesh: g: 32 (over z, y, x, core).
Axes of the slice: x: 2, y: 2, z: 4, core: 2. Of those that a mesh axis runs over, the one named last changes fastest.
Arguments:
- features: bfloat16 [65536, 128], P(None, 'g')
- w_self1: bfloat16 [128, 128], P('g')
- w_nbr1: bfloat16 [128, 128], P('g')
- nbr_ids: int32 [65536, 10], P('g')
- nbr_mask: int32 [65536, 10], P('g')
- w_self2: bfloat16 [128, 128], replicated
- w_nbr2: bfloat16 [128, 128], replicated
- w_self3: bfloat16 [128, 40], replicated
- w_nbr3: bfloat16 [128, 40], replicated
- labels: int32 [65536], P('g')
Outputs:
- output 1: float32 [], replicated
- output 2: float32 [128, 128], P('g')
- output 3: float32 [128, 128], P('g')
- output 4: float32 [128, 128], replicated
- output 5: float32 [128, 128], replicated
- output 6: float32 [128, 40], replicated
- output 7: float32 [128, 40], replicated
All inputs are finite; a program needn't handle non-finite values.
Results may differ from a plain program's by a relative error of at most 0.00265331.
Values are sent between devices in bfloat16 or wider.
A program may use at most 1 GiB of HBM per device.

v0:
```python
import jax
import jax.numpy as jnp
from jax import lax
from jax.sharding import PartitionSpec as P

GROUP_AXIS = 'g'


def neighbour_mean(table, nbr_ids, mask_f, degree):
    def body(running, slot_cols):
        ids_k, wts_k = slot_cols
        return running + wts_k[:, None] * table[ids_k].astype(jnp.float32), None

    start = jnp.zeros((nbr_ids.shape[0], table.shape[1]), jnp.float32)
    total, _ = lax.scan(body, start, (nbr_ids.T, mask_f.T))
    return total / degree[:, None]


def neighbour_mean_t(grads, nbr_ids, mask_f, degree, num_rows):
    scaled = grads.astype(jnp.float32) / degree[:, None]

    def body(running, slot_cols):
        ids_k, wts_k = slot_cols
        return running.at[ids_k].add(wts_k[:, None] * scaled), None

    start = jnp.zeros((num_rows, grads.shape[1]), jnp.float32)
    total, _ = lax.scan(body, start, (nbr_ids.T, mask_f.T))
    return total


def upper_layers(act_one, nbr_rows, mask_f, degree, w_self2, w_nbr2, w_self3, w_nbr3, label_rows, num_nodes):
    act_one_all = lax.all_gather(act_one, GROUP_AXIS, tiled=True)
    agg_one = neighbour_mean(act_one_all, nbr_rows, mask_f, degree).astype(jnp.bfloat16)
    pre_two = jnp.dot(act_one, w_self2, preferred_element_type=jnp.float32) + jnp.dot(agg_one, w_nbr2, preferred_element_type=jnp.float32)
    act_two = jnp.maximum(pre_two, 0.0).astype(jnp.bfloat16)
    act_two_all = lax.all_gather(act_two, GROUP_AXIS, tiled=True)
    agg_two = neighbour_mean(act_two_all, nbr_rows, mask_f, degree).astype(jnp.bfloat16)
    logits = jnp.dot(act_two, w_self3, preferred_element_type=jnp.float32) + jnp.dot(agg_two, w_nbr3, preferred_element_type=jnp.float32)
    log_norm = jax.nn.logsumexp(logits, axis=1)
    onehot = (label_rows[:, None] == jnp.arange(w_self3.shape[1])[None, :]).astype(jnp.float32)
    mean_loss = lax.psum(jnp.sum(log_norm - jnp.sum(onehot * logits, axis=1)), GROUP_AXIS) / num_nodes
    g_three = ((jnp.exp(logits - log_norm[:, None]) - onehot) / num_nodes).astype(jnp.bfloat16)
    grad_self3 = lax.psum(jnp.einsum('nh,nc->hc', act_two, g_three, preferred_element_type=jnp.float32), GROUP_AXIS)
    grad_nbr3 = lax.psum(jnp.einsum('nh,nc->hc', agg_two, g_three, preferred_element_type=jnp.float32), GROUP_AXIS)
    d_agg_two = jnp.einsum('nc,hc->nh', g_three, w_nbr3, preferred_element_type=jnp.float32).astype(jnp.bfloat16)
    back_two = lax.psum_scatter(neighbour_mean_t(d_agg_two, nbr_rows, mask_f, degree, num_nodes), GROUP_AXIS, scatter_dimension=0, tiled=True)
    d_act_two = jnp.einsum('nc,hc->nh', g_three, w_self3, preferred_element_type=jnp.float32) + back_two
    g_two = jnp.where(pre_two > 0, d_act_two, 0.0).astype(jnp.bfloat16)
    grad_self2 = lax.psum(jnp.einsum('nh,nj->hj', act_one, g_two, preferred_element_type=jnp.float32), GROUP_AXIS)
    grad_nbr2 = lax.psum(jnp.einsum('nh,nj->hj', agg_one, g_two, preferred_element_type=jnp.float32), GROUP_AXIS)
    d_agg_one = jnp.einsum('nj,hj->nh', g_two, w_nbr2, preferred_element_type=jnp.float32).astype(jnp.bfloat16)
    back_one = lax.psum_scatter(neighbour_mean_t(d_agg_one, nbr_rows, mask_f, degree, num_nodes), GROUP_AXIS, scatter_dimension=0, tiled=True)
    d_act_one = jnp.einsum('nj,hj->nh', g_two, w_self2, preferred_element_type=jnp.float32) + back_one
    return mean_loss, d_act_one, grad_self2, grad_nbr2, grad_self3, grad_nbr3


def solution(mesh):
    def device_step(feat_cols, w_self1_rows, w_nbr1_rows, nbr_rows, mask_rows, w_self2, w_nbr2, w_self3, w_nbr3, label_rows):
        num_nodes = feat_cols.shape[0]
        nbr_all = lax.all_gather(nbr_rows, GROUP_AXIS, tiled=True)
        mask_all = lax.all_gather(mask_rows, GROUP_AXIS, tiled=True).astype(jnp.float32)
        degree_all = jnp.sum(mask_all, axis=1)
        agg_x = neighbour_mean(feat_cols, nbr_all, mask_all, degree_all).astype(jnp.bfloat16)
        part_one = jnp.dot(feat_cols, w_self1_rows, preferred_element_type=jnp.float32) + jnp.dot(agg_x, w_nbr1_rows, preferred_element_type=jnp.float32)
        pre_one = lax.psum_scatter(part_one, GROUP_AXIS, scatter_dimension=0, tiled=True)
        act_one = jnp.maximum(pre_one, 0.0).astype(jnp.bfloat16)
        mask_f = mask_rows.astype(jnp.float32)
        degree = jnp.sum(mask_f, axis=1)
        mean_loss, d_act_one, grad_self2, grad_nbr2, grad_self3, grad_nbr3 = upper_layers(
            act_one, nbr_rows, mask_f, degree,
            w_self2, w_nbr2, w_self3, w_nbr3, label_rows, num_nodes)
        g_one = jnp.where(pre_one > 0, d_act_one, 0.0).astype(jnp.bfloat16)
        g_one_all = lax.all_gather(g_one, GROUP_AXIS, tiled=True)
        grad_self1 = jnp.einsum('nf,nh->fh', feat_cols, g_one_all, preferred_element_type=jnp.float32)
        grad_nbr1 = jnp.einsum('nf,nh->fh', agg_x, g_one_all, preferred_element_type=jnp.float32)
        return mean_loss, grad_self1, grad_nbr1, grad_self2, grad_nbr2, grad_self3, grad_nbr3

    row_spec = P(GROUP_AXIS, None)
    return jax.shard_map(
        device_step, mesh=mesh,
        in_specs=(P(None, GROUP_AXIS), row_spec, row_spec, row_spec, row_spec, P(), P(), P(), P(), P(GROUP_AXIS)),
        out_specs=(P(), row_spec, row_spec, P(), P(), P(), P()),
        check_vma=False)
```

profile of v0, /device:TPU:0, one launch (start us, length us, event | category | flops | bytes accessed | tf_op | source)
XLA Modules:
  0.0 5412.5 jit_solution(11948262914738356914)
XLA Ops:
  35.3 40.0 all-gather.6.cloned.1.call-done
  79.8 58.9 %all-gather.8.cloned.1.call-done = s32[65536,10]{0,1:T(8,128)} async-done(((s32[2048,10]{0,1:T(8,128)}), s32[65536,10]{0,1:T(8,128)}) %all-gather.8.cloned.1.call-update) | async-done | bytes 2621456 | tf_op jit(solution)/shard_map/all_gather | solution.py:60
  138.6 2616.8 %while.55 = (s32[]{:T(128)}, f32[65536,4]{1,0:T(8,128)}, f32[10,65536]{1,0:T(8,128)}, s32[10,65536]{1,0:T(8,128)}, bf16[65536,4]{1,0:T(8,128)(2,1)}, /*index=5*/s32[]{:T(128)}, s32[]{:T(128)}) while((s32[]{:T(128)}, f32[65536,4]{1,0:T(8,128)}, f32[10,65536]{1,0:T(8,128)}, s32[10,65536]{1,0:T(8,128)}, bf16[65536,4]{1,0:T(8,128)(2,1)}, ...), condition=%wide.region_1.2_spmd.clone, body=%wide.region_0.0_spmd.clone.sunk | while | flops 1310723 | bytes 5767263 | solution.py:15
  140.6 227.3 %gather_fusion = bf16[65536,4]{1,0:T(8,128)(2,1)} fusion(bf16[65536,4]{1,0:T(8,128)(2,1)} %get-tuple-element.447, s32[65536]{0:T(1024)S(1)} %broadcast_clamp_fusion.6), kind=kCustom, calls=%fused_computation.clone.clone.1 | custom fusion | bytes 1310720 | tf_op jit(solution)/shard_map/while/body/eval_jaxpr/gather | solution.py:12
  401.7 227.3 %gather_fusion = bf16[65536,4]{1,0:T(8,128)(2,1)} fusion(bf16[65536,4]{1,0:T(8,128)(2,1)} %get-tuple-element.447, s32[65536]{0:T(1024)S(1)} %broadcast_clamp_fusion.6), kind=kCustom, calls=%fused_computation.clone.clone.1 | custom fusion | bytes 1310720 | tf_op jit(solution)/shard_map/while/body/eval_jaxpr/gather | solution.py:12
  663.4 227.3 %gather_fusion = bf16[65536,4]{1,0:T(8,128)(2,1)} fusion(bf16[65536,4]{1,0:T(8,128)(2,1)} %get-tuple-element.447, s32[65536]{0:T(1024)S(1)} %broadcast_clamp_fusion.6), kind=kCustom, calls=%fused_computation.clone.clone.1 | custom fusion | bytes 1310720 | tf_op jit(solution)/shard_map/while/body/eval_jaxpr/gather | solution.py:12
  925.2 227.3 %gather_fusion = bf16[65536,4]{1,0:T(8,128)(2,1)} fusion(bf16[65536,4]{1,0:T(8,128)(2,1)} %get-tuple-element.447, s32[65536]{0:T(1024)S(1)} %broadcast_clamp_fusion.6), kind=kCustom, calls=%fused_computation.clone.clone.1 | custom fusion | bytes 1310720 | tf_op jit(solution)/shard_map/while/body/eval_jaxpr/gather | solution.py:12
  1186.9 227.3 %gather_fusion = bf16[65536,4]{1,0:T(8,128)(2,1)} fusion(bf16[65536,4]{1,0:T(8,128)(2,1)} %get-tuple-element.447, s32[65536]{0:T(1024)S(1)} %broadcast_clamp_fusion.6), kind=kCustom, calls=%fused_computation.clone.clone.1 | custom fusion | bytes 1310720 | tf_op jit(solution)/shard_map/while/body/eval_jaxpr/gather | solution.py:12
  1448.7 227.3 %gather_fusion = bf16[65536,4]{1,0:T(8,128)(2,1)} fusion(bf16[65536,4]{1,0:T(8,128)(2,1)} %get-tuple-element.447, s32[65536]{0:T(1024)S(1)} %broadcast_clamp_fusion.6), kind=kCustom, calls=%fused_computation.clone.clone.1 | custom fusion | bytes 1310720 | tf_op jit(solution)/shard_map/while/body/eval_jaxpr/gather | solution.py:12
  1710.4 227.3 %gather_fusion = bf16[65536,4]{1,0:T(8,128)(2,1)} fusion(bf16[65536,4]{1,0:T(8,128)(2,1)} %get-tuple-element.447, s32[65536]{0:T(1024)S(1)} %broadcast_clamp_fusion.6), kind=kCustom, calls=%fused_computation.clone.clone.1 | custom fusion | bytes 1310720 | tf_op jit(solution)/shard_map/while/body/eval_jaxpr/gather | solution.py:12
  1972.2 227.3 %gather_fusion = bf16[65536,4]{1,0:T(8,128)(2,1)} fusion(bf16[65536,4]{1,0:T(8,128)(2,1)} %get-tuple-element.447, s32[65536]{0:T(1024)S(1)} %broadcast_clamp_fusion.6), kind=kCustom, calls=%fused_computation.clone.clone.1 | custom fusion | bytes 1310720 | tf_op jit(solution)/shard_map/while/body/eval_jaxpr/gather | solution.py:12
  2233.9 227.3 %gather_fusion = bf16[65536,4]{1,0:T(8,128)(2,1)} fusion(bf16[65536,4]{1,0:T(8,128)(2,1)} %get-tuple-element.447, s32[65536]{0:T(1024)S(1)} %broadcast_clamp_fusion.6), kind=kCustom, calls=%fused_computation.clone.clone.1 | custom fusion | bytes 1310720 | tf_op jit(solution)/shard_map/while/body/eval_jaxpr/gather | solution.py:12
  2495.7 227.3 %gather_fusion = bf16[65536,4]{1,0:T(8,128)(2,1)} fusion(bf16[65536,4]{1,0:T(8,128)(2,1)} %get-tuple-element.447, s32[65536]{0:T(1024)S(1)} %broadcast_clamp_fusion.6), kind=kCustom, calls=%fused_computation.clone.clone.1 | custom fusion | bytes 1310720 | tf_op jit(solution)/shard_map/while/body/eval_jaxpr/gather | solution.py:12
  2817.7 353.2 %reduce-scatter.4.cloned.1.call-done = f32[2048,128]{1,0:T(8,128)} async-done(((f32[65536,128]{1,0:T(8,128)}), f32[2048,128]{1,0:T(8,128)}) %reduce-scatter.4.cloned.1.call-update) | async-done | bytes 1048592 | tf_op jit(solution)/shard_map/reduce_scatter | solution.py:65
  3175.4 119.8 %all-gather.10.cloned.1.call-done = bf16[65536,128]{1,0:T(8,128)(2,1)} async-done(((bf16[2048,128]{1,0:T(8,128)(2,1)}), bf16[65536,128]{1,0:T(8,128)(2,1)}) %all-gather.10.cloned.1.call-update) | async-done | bytes 16777232 | tf_op jit(solution)/shard_map/all_gather | solution.py:32
  3295.3 148.9 %while.56 = (s32[]{:T(128)}, f32[2048,128]{1,0:T(8,128)S(1)}, f32[10,2048]{1,0:T(8,128)S(1)}, s32[10,2048]{1,0:T(8,128)}, bf16[65536,128]{1,0:T(8,128)(2,1)}, /*index=5*/s32[]{:T(128)}, s32[]{:T(128)}) while((s32[]{:T(128)}, f32[2048,128]{1,0:T(8,128)S(1)}, f32[10,2048]{1,0:T(8,128)S(1)}, s32[10,2048]{1,0:T(8,128)}, ...), condition=%wide.region_5.6_spmd.clone, body=%wide.region_4.5_spmd.clone.sunk | while | flops 1056771 | bytes 3735647 | solution.py:15
  3449.2 111.2 %all-gather.12.cloned.1.call-done = bf16[65536,128]{1,0:T(8,128)(2,1)} async-done(((bf16[2048,128]{1,0:T(8,128)(2,1)}), bf16[65536,128]{1,0:T(8,128)(2,1)}) %all-gather.12.cloned.1.call-update) | async-done | bytes 16777232 | tf_op jit(solution)/shard_map/all_gather | solution.py:36
  3560.4 148.9 %while.57 = (s32[]{:T(128)}, f32[2048,128]{1,0:T(8,128)S(1)}, f32[10,2048]{1,0:T(8,128)S(1)}, s32[10,2048]{1,0:T(8,128)}, bf16[65536,128]{1,0:T(8,128)(2,1)}, /*index=5*/s32[]{:T(128)}, s32[]{:T(128)}) while((s32[]{:T(128)}, f32[2048,128]{1,0:T(8,128)S(1)}, f32[10,2048]{1,0:T(8,128)S(1)}, s32[10,2048]{1,0:T(8,128)}, ...), condition=%wide.region_8.9_spmd.clone, body=%wide.region_7.8_spmd.clone.sunk | while | flops 1056771 | bytes 3735647 | solution.py:15
  3723.1 346.4 %while.53 = (s32[]{:T(128)}, f32[65536,128]{1,0:T(8,128)}, s32[10,2048]{1,0:T(8,128)}, f32[10,2048]{1,0:T(8,128)}, f32[2048,128]{1,0:T(8,128)S(1)}, /*index=5*/s32[]{:T(128)}) while((s32[]{:T(128)}, f32[65536,128]{1,0:T(8,128)}, s32[10,2048]{1,0:T(8,128)}, f32[10,2048]{1,0:T(8,128)}, f32[2048,128]{1,0:T(8,128)S(1)}, ...), condition=%wide.region_16.17_spmd, body=%wide.region_14.16_spmd.sunk | while | flops 530434 | bytes 34644044 | solution.py:27
  3759.5 32.9 scatter_custom_fusion.9
  3794.1 32.9 scatter_custom_fusion.9
  3863.4 32.9 scatter_custom_fusion.9
  3932.7 32.9 scatter_custom_fusion.9
  4001.9 32.9 scatter_custom_fusion.9
  4036.6 32.9 scatter_custom_fusion.9
  4069.8 352.6 %reduce-scatter.6.cloned.1.call-done = f32[2048,128]{1,0:T(8,128)} async-done(((f32[65536,128]{1,0:T(8,128)}), f32[2048,128]{1,0:T(8,128)}) %reduce-scatter.6.cloned.1.call-update) | async-done | bytes 1048592 | tf_op jit(solution)/shard_map/reduce_scatter | solution.py:46
  4435.4 346.4 %while.54 = (s32[]{:T(128)}, f32[65536,128]{1,0:T(8,128)}, s32[10,2048]{1,0:T(8,128)}, f32[10,2048]{1,0:T(8,128)}, f32[2048,128]{1,0:T(8,128)S(1)}, /*index=5*/s32[]{:T(128)}) while((s32[]{:T(128)}, f32[65536,128]{1,0:T(8,128)}, s32[10,2048]{1,0:T(8,128)}, f32[10,2048]{1,0:T(8,128)}, f32[2048,128]{1,0:T(8,128)S(1)}, ...), condition=%wide.region_20.21_spmd, body=%wide.region_18.20_spmd.sunk | while | flops 530434 | bytes 34644044 | solution.py:27
  4471.8 32.9 scatter_custom_fusion.11
  4781.9 362.0 %reduce-scatter.8.cloned.1.call-done = f32[2048,128]{1,0:T(8,128)} async-done(((f32[65536,128]{1,0:T(8,128)}), f32[2048,128]{1,0:T(8,128)}) %reduce-scatter.8.cloned.1.call-update) | async-done | bytes 1048592 | tf_op jit(solution)/shard_map/reduce_scatter | solution.py:52
  5147.0 49.1 all-reduce
  5198.7 70.7 %all-gather.14.cloned.1.call-done = bf16[65536,128]{1,0:T(8,128)(2,1)} async-done(((bf16[2048,128]{1,0:T(8,128)(2,1)}), bf16[65536,128]{1,0:T(8,128)(2,1)}) %all-gather.14.cloned.1.call-update) | async-done | bytes 16777232 | tf_op jit(solution)/shard_map/all_gather | solution.py:73
  5290.4 111.5 %all-reduce.4.cloned.1.call-done = (f32[128,128]{1,0:T(8,128)}, f32[128,128]{1,0:T(8,128)}) async-done(((f32[128,128]{1,0:T(8,128)}, f32[128,128]{1,0:T(8,128)}), (f32[128,128]{1,0:T(8,128)}, f32[128,128]{1,0:T(8,128)})) %all-reduce.4.cloned.1.call-update) | async-done | bytes 131088 | tf_op jit(solution)/shard_map/psum | solution.py:49
  (275 shorter events, 1262.7 us)
Async XLA Ops:
  7.2 3438.2 %copy-start = (bf16[128,128]{1,0:T(8,128)(2,1)S(1)}, bf16[128,128]{1,0:T(8,128)(2,1)}, u32[]{:S(2)}) copy-start(bf16[128,128]{1,0:T(8,128)(2,1)} %param.26) | copy-start | bytes 98308
  7.2 68.2 %all-gather.6.cloned.1.call-start = ((), (), s32[]{:S(2)}) async-start(), calls=%async_computation.3 | async-start | bytes 4325376 | tf_op jit(solution)/shard_map/all_gather | solution.py:61
  7.9 130.7 %all-gather.8.cloned.1.call-start = ((), (), s32[]{:S(2)}) async-start(), calls=%async_computation.4 | async-start | bytes 4325376 | tf_op jit(solution)/shard_map/all_gather | solution.py:60
  8.7 3162.2 %reduce-scatter.4.cloned.1.call-start = ((), (), s32[]{:S(2)}) async-start(), calls=%async_computation.5 | async-start | bytes 34603008 | tf_op jit(solution)/shard_map/reduce_scatter | solution.py:65
  2755.5 33.1 copy-start.13
  2817.6 355.4 %copy-start.6 = (s32[2048,10]{0,1:T(8,128)S(1)}, s32[2048,10]{0,1:T(8,128)}, u32[]{:S(2)}) copy-start(s32[2048,10]{0,1:T(8,128)} %param.24) | copy-start | bytes 245764
  2817.6 355.5 %copy-start.8 = (bf16[128,128]{1,0:T(8,128)(2,1)S(1)}, bf16[128,128]{1,0:T(8,128)(2,1)}, u32[]{:S(2)}) copy-start(bf16[128,128]{1,0:T(8,128)(2,1)} %param.25) | copy-start | bytes 98308
  2817.6 630.2 %copy-start.10 = (bf16[128,40]{0,1:T(8,128)(2,1)S(1)}, bf16[128,40]{0,1:T(8,128)(2,1)}, u32[]{:S(2)}) copy-start(bf16[128,40]{0,1:T(8,128)(2,1)} %param.27) | copy-start | bytes 30724
  2817.6 477.6 %all-gather.10.cloned.1.call-start = ((), (), s32[]{:S(2)}) async-start(), calls=%async_computation.6 | async-start | bytes 17301504 | tf_op jit(solution)/shard_map/all_gather | solution.py:32
  3173.0 387.4 %all-gather.12.cloned.1.call-start = ((), (), s32[]{:S(2)}) async-start(), calls=%async_computation.7 | async-start | bytes 17301504 | tf_op jit(solution)/shard_map/all_gather | solution.py:36
  3295.3 415.0 %copy-start.12 = (bf16[128,40]{0,1:T(8,128)(2,1)S(1)}, bf16[128,40]{0,1:T(8,128)(2,1)}, u32[]{:S(2)}) copy-start(bf16[128,40]{0,1:T(8,128)(2,1)} %param.28) | copy-start | bytes 30724
  3295.3 415.5 %copy-start.11 = (s32[2048]{0:T(1024)S(1)}, s32[2048]{0:T(1024)}, u32[]{:S(2)}) copy-start(s32[2048]{0:T(1024)} %param.29) | copy-start | bytes 24580
  3444.6 0.8 copy-start.4
  3447.7 974.7 %reduce-scatter.6.cloned.1.call-start = ((), (), s32[]{:S(2)}) async-start(), calls=%async_computation.8 | async-start | bytes 34603008 | tf_op jit(solution)/shard_map/reduce_scatter | solution.py:46
  3709.3 0.6 copy-start.7
  4069.5 1074.4 %reduce-scatter.8.cloned.1.call-start = ((), (), s32[]{:S(2)}) async-start(), calls=%async_computation.9 | async-start | bytes 34603008 | tf_op jit(solution)/shard_map/reduce_scatter | solution.py:52
  4781.8 362.1 %copy-start.9 = (bf16[128,128]{1,0:T(8,128)(2,1)S(1)}, bf16[128,128]{1,0:T(8,128)(2,1)}, u32[]{:S(2)}) copy-start(bf16[128,128]{1,0:T(8,128)(2,1)} %param.25) | copy-start | bytes 98308
  4781.8 365.0 %copy-start.2 = (bf16[2048,128]{1,0:T(8,128)(2,1)S(1)}, bf16[2048,128]{1,0:T(8,128)(2,1)}, u32[]{:S(2)}) copy-start(bf16[2048,128]{1,0:T(8,128)(2,1)} %get-tuple-element.270) | copy-start | bytes 1572868
  4781.8 415.0 %copy-start.5 = (bf16[2048,128]{1,0:T(8,128)(2,1)S(1)}, bf16[2048,128]{1,0:T(8,128)(2,1)}, u32[]{:S(2)}) copy-start(bf16[2048,128]{1,0:T(8,128)(2,1)} %copy-done.4) | copy-start | bytes 1572868
  4781.8 416.0 %copy-start.1 = (bf16[2048,128]{1,0:T(8,128)(2,1)S(1)}, bf16[2048,128]{1,0:T(8,128)(2,1)}, u32[]{:S(2)}) copy-start(bf16[2048,128]{1,0:T(8,128)(2,1)} %maximum_convert_fusion.1) | copy-start | bytes 1572868
  4781.8 501.0 %copy-start.3 = (bf16[65536,4]{0,1:T(4,128)(2,1)S(1)}, bf16[65536,4]{0,1:T(4,128)(2,1)}, u32[]{:S(2)}) copy-start(bf16[65536,4]{0,1:T(4,128)(2,1)} %param.20) | copy-start | bytes 1572868
  4781.8 487.6 %all-gather.14.cloned.1.call-start = ((), (), s32[]{:S(2)}) async-start(), calls=%async_computation.10 | async-start | bytes 17301504 | tf_op jit(solution)/shard_map/all_gather | solution.py:73
  5146.6 255.4 %all-reduce.4.cloned.1.call-start = ((), (), s32[]{:S(2)}) async-start(), calls=%async_computation.11 | async-start | bytes 262144 | tf_op jit(solution)/shard_map/psum | solution.py:49
Sparse Core Ops, SparseCore 0:
  10.9 64.4 all-gather.5
  78.2 60.3 all-gather.7
  2817.8 353.0 reduce-scatter.3
  3173.6 121.6 all-gather.9
  3447.9 112.4 all-gather.11
  4069.6 352.7 reduce-scatter.5
  4781.9 361.8 reduce-scatter.7
  5146.7 122.6 all-gather.13
  5275.7 126.1 all-reduce.3
where the time goes:
time: 5420 us; the launch traced here: 5410 us
  local copies, waits for them, and re-layouts  2620 us (48%)
  waiting for transfers between devices  1580 us (29%)
  other arithmetic  1070 us (20%)
  matrix products  79.1 us (1%)
    gather x30, local copies, waits for them, and re-layouts, body(): return (running + wts_k[:, None] * table[ids_k].astype(jnp.float32), None)  2540 us
    scatter-add x20, other arithmetic, body(): return (running.at[ids_k].add(wts_k[:, None] * scaled), None)  658 us
    reduce_scatter x1, waiting for transfers between devices, upper_layers(): lax.psum_scatter(neighbour_mean_t(d_agg_one, nbr_rows, mask_f, degree, nu...  362 us
    reduce_scatter x1, waiting for transfers between devices, device_step(): lax.psum_scatter(part_one, GROUP_AXIS, scatter_dimension=0, tiled=True)  353 us
    reduce_scatter x1, waiting for transfers between devices, upper_layers(): lax.psum_scatter(neighbour_mean_t(d_agg_two, nbr_rows, mask_f, degree, nu...  353 us
    add x30, other arithmetic, body(): return (running + wts_k[:, None] * table[ids_k].astype(jnp.float32), None)  315 us
    all_gather x1, waiting for transfers between devices, upper_layers(): act_one_all = lax.all_gather(act_one, GROUP_AXIS, tiled=True)  120 us
    psum x1, waiting for transfers between devices, upper_layers(): lax.psum(jnp.einsum('nh,nj->hj', act_one, g_two, preferred_element_type=j...  112 us
  transfers between devices with their start and end apart: 9, of which 9 were waited for; matrix products, arithmetic and copies ran while one was open for 1% of the time, Pallas kernels for 0%

commit v1 on v0

v1 whole, which is shorter than its diff:
```python
import functools

import jax
import jax.numpy as jnp
from jax import lax
from jax.experimental import pallas as pl
from jax.experimental.pallas import tpu as pltpu
from jax.sharding import PartitionSpec as P

AX = 'g'
N = 65536
R = 2048
D = 128
K = 10
C = 40
NDEV = 32
NQ = 8
NBQ = 2
E = R * K
CAP = 2048
NACC = 8
MESH = pl.DeviceIdType.MESH
VMEM = pltpu.VMEM
BF = jnp.bfloat16
F32 = jnp.float32
VLIM = 62 * 1024 * 1024


def gather_blocks(x_ref, tab, lsem, rsem, ssem, csem, rb, arrived=None):
    cr = rb // NQ
    me = lax.axis_index(AX)
    z, y, x, c = me // 8, lax.rem(me // 4, 2), lax.rem(me // 2, 2), lax.rem(me, 2)

    def dev(z_, y_, x_, c_):
        return ((z_ * 2 + y_) * 2 + x_) * 2 + c_

    d_x, d_y, d_up, d_dn, d_c = dev(z, y, 1 - x, c), dev(z, 1 - y, x, c), me + 8, me - 8, dev(z, y, x, 1 - c)
    bar = pltpu.get_barrier_semaphore()
    for d in (d_x, d_y, d_c):
        pl.semaphore_signal(bar, inc=1, device_id=(d,), device_id_type=MESH)

    @pl.when(z < 3)
    def _():
        pl.semaphore_signal(bar, inc=1, device_id=(d_up,), device_id_type=MESH)

    @pl.when(z > 0)
    def _():
        pl.semaphore_signal(bar, inc=1, device_id=(d_dn,), device_id_type=MESH)

    pl.semaphore_wait(bar, 4 + lax.rem(z + 1, 4) // 2)

    def rows(zo, yo, xo, q):
        return pl.ds(pl.multiple_of(dev(zo, yo, xo, c) * rb + q * cr, cr), cr)

    def slot(zo, yo, xo, q):
        return ((zo * 2 + yo) * 2 + xo) * NQ + q

    def send(d, src, dst, ss, rs):
        pltpu.make_async_remote_copy(
            src_ref=src, dst_ref=dst, send_sem=ss, recv_sem=rs, device_id=(d,), device_id_type=MESH).start()

    def forward(zo, yo, xo, q, up, dn, to_x, to_y, src=None):
        dst = tab.at[rows(zo, yo, xo, q)]
        src = dst if src is None else src
        rs = rsem.at[slot(zo, yo, xo, q)]
        if up is not None:
            @pl.when(up)
            def _():
                send(d_up, src, dst, ssem.at[0], rs)

            @pl.when(dn)
            def _():
                send(d_dn, src, dst, ssem.at[1], rs)
        if to_x:
            send(d_x, src, dst, ssem.at[2], rs)
        if to_y:
            send(d_y, src, dst, ssem.at[3], rs)
        send(d_c, src, dst, csem.at[0], csem.at[1])

    for q in range(NQ):
        forward(z, y, x, q, z < 3, z > 0, True, True, x_ref.at[pl.ds(q * cr, cr)])
    own = pltpu.make_async_copy(x_ref, tab.at[pl.ds(pl.multiple_of(me * rb, rb), rb)], lsem)
    own.start()
    zr = [z, z + 1 - 2 * lax.rem(z, 2), 2 - z // 2, 3 - 3 * (z // 2)]

    def handle(kind, r, q, first, par):
        zo = zr[r]
        yo = 1 - y if kind in 'YD' else y
        xo = 1 - x if kind in 'XD' else x
        here = tab.at[rows(zo, yo, xo, q)]
        pltpu.make_async_remote_copy(
            src_ref=here, dst_ref=here, send_sem=ssem.at[0], recv_sem=rsem.at[slot(zo, yo, xo, q)],
            device_id=(d_x,), device_id_type=MESH).wait_recv()
        up = dn = None
        if kind == 'C' or first:
            up, dn = (z < 3, z > 0) if r == 0 else ((zo < z) & (z < 3), (zo > z) & (z > 0))
        col = kind == 'C' and not first
        over = not first or r == 0
        forward(zo, yo, xo, q, up, dn,
                col or (kind == 'Y' and par == 1 and over), col or (kind == 'X' and par == 0 and over))
        if arrived is not None:
            arrived(dev(zo, yo, xo, c) * rb + q * cr, cr)

    for s in range(5):
        groups = []
        if s < 3:
            groups.append(('C', s + 1))
        if s < 4:
            groups += [('X', s), ('Y', s)]
        if s > 0:
            groups.append(('D', s - 1))
        for q in range(NBQ):
            for kind, r in groups:
                handle(kind, r, q, True, q % 2)

        def pair(p, _, groups=groups):
            for par in range(2):
                for kind, r in groups:
                    handle(kind, r, NBQ + 2 * p + par, False, par)
            return 0

        lax.fori_loop(0, (NQ - NBQ) // 2, pair, 0)

    def wait_chunks(n, sem):
        v = tab.at[pl.ds(0, n * cr)]
        pltpu.make_async_copy(v, v, sem).wait()

    own.wait()
    na = NQ - NBQ
    flat = 4 * na + 4 * (na // 2) + NBQ + NBQ // 2
    wait_chunks(flat, ssem.at[2])
    wait_chunks(flat, ssem.at[3])
    for k in range(3):
        @pl.when(z == k)
        def _(k=k):
            wait_chunks((k + 1) * (na + 4 * NBQ), ssem.at[0])

        @pl.when(z == 3 - k)
        def _(k=k):
            wait_chunks((k + 1) * (na + 4 * NBQ), ssem.at[1])
    wait_chunks(16 * NQ, csem.at[0])
    wait_chunks(16 * NQ, csem.at[1])


AG_SEMS = [pltpu.SemaphoreType.DMA, pltpu.SemaphoreType.DMA((16 * NQ,)), pltpu.SemaphoreType.DMA((4,)),
           pltpu.SemaphoreType.DMA((2,))]


def all_gather(v, cid, name):
    rb = v.shape[0]

    def kernel(x_ref, o_ref, lsem, rsem, ssem, csem):
        gather_blocks(x_ref, o_ref, lsem, rsem, ssem, csem, rb)

    return pl.pallas_call(
        kernel, out_shape=jax.ShapeDtypeStruct((rb * NDEV,) + v.shape[1:], v.dtype),
        in_specs=[pl.BlockSpec(memory_space=VMEM)], out_specs=pl.BlockSpec(memory_space=pl.ANY),
        scratch_shapes=AG_SEMS, name=name,
        compiler_params=pltpu.CompilerParams(collective_id=cid, has_side_effects=True))(v)


def dot(a, b):
    return jnp.dot(a, b, preferred_element_type=F32)


def dot_rows(a, b):
    return lax.dot_general(a, b, (((0,), (0,)), ((), ())), preferred_element_type=F32)


def dot_t(a, b):
    return lax.dot_general(a, b, (((1,), (1,)), ((), ())), preferred_element_type=F32)


CB = 256


def load_table(tab_hbm, tab, stg, tsem):
    nb, ch = stg.shape[0], stg.shape[1]

    def tcopy(i, s):
        return pltpu.make_async_copy(tab_hbm.at[pl.ds(pl.multiple_of(i * ch, ch), ch), :], stg.at[s], tsem.at[s])

    for s in range(nb - 1):
        tcopy(s, s).start()

    def conv(i, _):
        s = lax.rem(i, nb)
        tcopy(i, s).wait()

        @pl.when(i + nb - 1 < N // ch)
        def _():
            tcopy(i + nb - 1, lax.rem(i + nb - 1, nb)).start()

        tab[pl.ds(pl.multiple_of(i * ch, ch), ch), :] = stg[s].astype(F32)
        return 0

    lax.fori_loop(0, N // ch, conv, 0)


def table_mean(tab_hbm, idx_ref, tab, stg, acc, tsem):
    load_table(tab_hbm, tab, stg, tsem)
    tab[pl.ds(N, 8), :] = jnp.zeros((8, D), F32)

    def body(b, _):
        for u in range(8):
            r = b * 8 + u
            v = [tab[pl.ds(idx_ref[k * R + r], 1), :] for k in range(K)]
            while len(v) > 1:
                v = [v[j] + v[j + 1] if j + 1 < len(v) else v[j] for j in range(0, len(v), 2)]
            acc[pl.ds(r, 1), :] = v[0]
        return 0

    lax.fori_loop(0, R // 8, body, 0)


TABLE = [VMEM((N + 8, D), F32), VMEM((4, 1024, D), BF), VMEM((R, D), F32), pltpu.SemaphoreType.DMA((4,))]


def hidden_layer(v, idx, deg, w_self, w_nbr, name):
    def kernel(idx_ref, tab_hbm, x_ref, deg_ref, ws_ref, wn_ref, agg_ref, pre_ref, act_ref, tab, stg, acc, tsem):
        table_mean(tab_hbm, idx_ref, tab, stg, acc, tsem)

        def block(i, _):
            r = pl.ds(pl.multiple_of(i * CB, CB), CB)
            agg = (acc[r, :] / deg_ref[r, :]).astype(BF)
            agg_ref[r, :] = agg
            pre = dot(x_ref[r, :], ws_ref[...]) + dot(agg, wn_ref[...])
            pre_ref[r, :] = pre
            act_ref[r, :] = jnp.maximum(pre, 0.0).astype(BF)
            return 0

        lax.fori_loop(0, R // CB, block, 0)

    vm = pl.BlockSpec(memory_space=VMEM)
    return pl.pallas_call(
        kernel, name=name,
        out_shape=[jax.ShapeDtypeStruct((R, D), BF), jax.ShapeDtypeStruct((R, D), F32), jax.ShapeDtypeStruct((R, D), BF)],
        in_specs=[pl.BlockSpec(memory_space=pltpu.SMEM), pl.BlockSpec(memory_space=pl.ANY), vm, vm, vm, vm],
        out_specs=[vm] * 3, scratch_shapes=TABLE, compiler_params=pltpu.CompilerParams(vmem_limit_bytes=VLIM),
    )(idx, all_gather(v, 2, 'gather_rows'), v, deg, w_self, w_nbr)


def output_layer(v, idx, deg, labels, w_self, w_nbr, name):
    def kernel(idx_ref, tab_hbm, x_ref, deg_ref, lab_ref, ws_ref, wn_ref, g_ref, u_ref, dws_ref, dwn_ref, loss_ref,
               tab, stg, acc, tsem):
        table_mean(tab_hbm, idx_ref, tab, stg, acc, tsem)
        dws_ref[...] = jnp.zeros((D, D), F32)
        dwn_ref[...] = jnp.zeros((D, D), F32)
        lane = lax.broadcasted_iota(jnp.int32, (CB, D), 1)

        def block(i, loss):
            r = pl.ds(pl.multiple_of(i * CB, CB), CB)
            act = x_ref[r, :]
            agg = (acc[r, :] / deg_ref[r, :]).astype(BF)
            logits = dot(act, ws_ref[...]) + dot(agg, wn_ref[...])
            live = lane < C
            top = jnp.max(jnp.where(live, logits, -jnp.inf), axis=1, keepdims=True)
            ex = jnp.where(live, jnp.exp(logits - top), 0.0)
            norm = top + jnp.log(jnp.sum(ex, axis=1, keepdims=True))
            hot = jnp.where(lane == lab_ref[r, :], 1.0, 0.0)
            loss = loss + jnp.sum(jnp.where(live, hot * (norm - logits), 0.0))
            prob = jnp.where(live, jnp.exp(logits - norm), 0.0)
            g = ((prob - hot) / N).astype(BF)
            g_ref[r, :] = g
            u_ref[r, :] = dot_t(g, wn_ref[...]).astype(BF)
            dws_ref[...] += dot_rows(act, g)
            dwn_ref[...] += dot_rows(agg, g)
            return loss

        loss = lax.fori_loop(0, R // CB, block, jnp.float32(0.0))
        loss_ref[...] = jnp.full((8, D), loss, F32)

    vm = pl.BlockSpec(memory_space=VMEM)
    return pl.pallas_call(
        kernel, name=name,
        out_shape=[jax.ShapeDtypeStruct((R, D), BF), jax.ShapeDtypeStruct((R, D), BF),
                   jax.ShapeDtypeStruct((D, D), F32), jax.ShapeDtypeStruct((D, D), F32), jax.ShapeDtypeStruct((8, D), F32)],
        in_specs=[pl.BlockSpec(memory_space=pltpu.SMEM), pl.BlockSpec(memory_space=pl.ANY)] + [vm] * 5,
        out_specs=[vm] * 5, scratch_shapes=TABLE, compiler_params=pltpu.CompilerParams(vmem_limit_bytes=VLIM),
    )(idx, all_gather(v, 2, 'gather_rows'), v, deg, labels, w_self, w_nbr)


def table_mean_t(lo_ref, hi_ref, src_hbm, dst_hbm, wt_hbm, tab_hbm, tab, stg, accs, lists, tsem, lsem):
    src, dst, wt = lists

    def list_copies(s, part, slot):
        off = pl.multiple_of(s * E + (lo_ref[s] // 1024) * 1024 + part * CAP, 1024)
        return [pltpu.make_async_copy(h.at[pl.ds(off, CAP)], b.at[pl.ds(pl.multiple_of(slot * CAP, CAP), CAP)], lsem.at[j, slot])
                for j, (h, b) in enumerate(((src_hbm, src), (dst_hbm, dst), (wt_hbm, wt)))]

    for cp in list_copies(0, 0, 0):
        cp.start()

    load_table(tab_hbm, tab, stg, tsem)
    for a in accs:
        a[...] = jnp.zeros(a.shape, F32)

    def run(slot, first, last):
        def body(b, _):
            for u in range(NACC):
                e = slot * CAP + b * NACC + u
                d = pl.ds(dst[e], 1)
                accs[u][d, :] += tab[pl.ds(src[e], 1), :] * wt[e]
            return 0

        lax.fori_loop(first // NACC, (last + NACC - 1) // NACC, body, 0)

    def sender(s, _):
        slot = lax.rem(s, 2)
        for cp in list_copies(s, 0, slot):
            cp.wait()

        @pl.when(s + 1 < NDEV)
        def _():
            for cp in list_copies(s + 1, 0, 1 - slot):
                cp.start()

        base = (lo_ref[s] // 1024) * 1024
        run(slot, lo_ref[s] - base, jnp.minimum(hi_ref[s] - base, CAP))

        def more(p, _):
            for cp in list_copies(s, p, slot):
                cp.start()
            for cp in list_copies(s, p, slot):
                cp.wait()
            run(slot, 0, jnp.minimum(hi_ref[s] - base - p * CAP, CAP))
            return 0

        lax.fori_loop(1, (hi_ref[s] - base + CAP - 1) // CAP, more, 0)
        return 0

    lax.fori_loop(0, NDEV, sender, 0)


def backward_layer(table, lo, hi, lists, g_up, w_self, pre, act, agg, w_nbr, name):
    last = w_nbr is None

    def kernel(lo_ref, hi_ref, src_hbm, dst_hbm, wt_hbm, tab_hbm, gu_ref, ws_ref, pre_ref, act_ref, agg_ref, *rest):
        if last:
            dws_ref, dwn_ref = rest[:2]
            rest = rest[2:]
        else:
            wn_ref, g_ref, u_ref, dws_ref, dwn_ref = rest[:5]
            rest = rest[5:]
        tab, stg = rest[:2]
        accs = rest[2:2 + NACC]
        src, dst, wt, tsem, lsem = rest[2 + NACC:]
        table_mean_t(lo_ref, hi_ref, src_hbm, dst_hbm, wt_hbm, tab_hbm, tab, stg, accs, (src, dst, wt), tsem, lsem)
        dws_ref[...] = jnp.zeros((D, D), F32)
        dwn_ref[...] = jnp.zeros((D, D), F32)

        def block(i, _):
            r = pl.ds(pl.multiple_of(i * CB, CB), CB)
            back = [a[r, :] for a in accs]
            while len(back) > 1:
                back = [back[j] + back[j + 1] for j in range(0, len(back), 2)]
            d_act = dot_t(gu_ref[r, :], ws_ref[...]) + back[0]
            g = jnp.where(pre_ref[r, :] > 0, d_act, 0.0).astype(BF)
            dws_ref[...] += dot_rows(act_ref[r, :], g)
            dwn_ref[...] += dot_rows(agg_ref[r, :], g)
            if not last:
                g_ref[r, :] = g
                u_ref[r, :] = dot_t(g, wn_ref[...]).astype(BF)
            return 0

        lax.fori_loop(0, R // CB, block, 0)

    vm, sm, hb = (pl.BlockSpec(memory_space=m) for m in (VMEM, pltpu.SMEM, pl.ANY))
    outs = [jax.ShapeDtypeStruct((D, D), F32)] * 2
    args = [lo, hi, *lists, table, g_up, w_self, pre, act, agg]
    specs = [sm, sm, hb, hb, hb, hb, vm, vm, vm, vm, vm]
    if not last:
        outs = [jax.ShapeDtypeStruct((R, D), BF)] * 2 + outs
        args.append(w_nbr)
        specs.append(vm)
    return pl.pallas_call(
        kernel, name=name, out_shape=outs, in_specs=specs, out_specs=[vm] * len(outs),
        scratch_shapes=[VMEM((N, D), F32), VMEM((4, 1024, D), BF)] + [VMEM((R + 8, D), F32)] * NACC
        + [pltpu.SMEM((2 * CAP,), jnp.int32), pltpu.SMEM((2 * CAP,), jnp.int32), pltpu.SMEM((2 * CAP,), F32),
           pltpu.SemaphoreType.DMA((4,)), pltpu.SemaphoreType.DMA((3, 2))],
        compiler_params=pltpu.CompilerParams(vmem_limit_bytes=VLIM))(*args)


def in_edges(nbr_t, mask_t, deg, cid):
    me = lax.axis_index(AX)
    live = mask_t > 0
    here = jnp.arange(R, dtype=jnp.int32)[None, :]
    key = jnp.where(live, nbr_t * 32768 + here * 16 + deg[None, :], -1)
    key = lax.sort(key.reshape(E))
    bounds = jnp.arange(NDEV + 1, dtype=jnp.int32)
    starts = jnp.sum(((key >> 26)[None, :] < bounds[:, None]).astype(jnp.int32), axis=1)
    pay = jnp.concatenate([key.reshape(E // D, D), jnp.pad(starts[None, :], ((0, 31), (0, D - NDEV - 1)))])
    every = all_gather(pay, cid, 'gather_edges').reshape(NDEV, E // D + 32, D)
    keys = every[:, :E // D].reshape(NDEV, E)
    sender = jnp.arange(NDEV, dtype=jnp.int32)[:, None]
    src = ((keys >> 4) & (R - 1)) + sender * R
    dst = (keys >> 15) - me * R
    dst = jnp.where((dst < 0) | (dst >= R) | (keys < 0), R, dst)
    wt = 1.0 / jnp.maximum(keys & 15, 1).astype(F32)
    pad = lambda v: jnp.pad(v.reshape(-1), (0, CAP))
    marks = every[:, E // D, :NDEV + 1]
    lo = lax.dynamic_index_in_dim(marks, me, 1, keepdims=False)
    hi = lax.dynamic_index_in_dim(marks, me + 1, 1, keepdims=False)
    return lo, hi, (pad(src), pad(dst), pad(wt))


RED = 24


def reduce_shares(parts, cid):
    def kernel(p_ref, own_ref, all_ref, got, mine, rsem, ssem, lsem):
        me = lax.axis_index(AX)
        bar = pltpu.get_barrier_semaphore()

        def greet(k, _):
            pl.semaphore_signal(bar, inc=1, device_id=(lax.rem(me + k, NDEV),), device_id_type=MESH)
            return 0

        lax.fori_loop(1, NDEV, greet, 0)
        pl.semaphore_wait(bar, NDEV - 1)

        def share(k, _):
            d = lax.rem(me + k, NDEV)
            pltpu.make_async_remote_copy(
                src_ref=p_ref.at[d], dst_ref=got.at[me], send_sem=ssem.at[0], recv_sem=rsem.at[0],
                device_id=(d,), device_id_type=MESH).start()
            return 0

        lax.fori_loop(1, NDEV, share, 0)
        own = pltpu.make_async_copy(p_ref.at[me], got.at[me], lsem.at[0])
        own.start()
        own.wait()
        most = got.at[pl.ds(0, NDEV - 1)]
        pltpu.make_async_copy(most, most, rsem.at[0]).wait()
        v = [got[d] for d in range(NDEV)]
        while len(v) > 1:
            v = [v[j] + v[j + 1] for j in range(0, len(v), 2)]
        own_ref[...] = v[0][:8]
        mine[...] = v[0][8:]

        def tell(k, _):
            d = lax.rem(me + k, NDEV)
            pltpu.make_async_remote_copy(
                src_ref=mine, dst_ref=all_ref.at[me], send_sem=ssem.at[1], recv_sem=rsem.at[1],
                device_id=(d,), device_id_type=MESH).start()
            return 0

        lax.fori_loop(1, NDEV, tell, 0)
        keep = pltpu.make_async_copy(mine, all_ref.at[me], lsem.at[1])
        keep.start()
        keep.wait()
        most = all_ref.at[pl.ds(0, NDEV - 1)]
        pltpu.make_async_copy(most, most, rsem.at[1]).wait()
        pltpu.make_async_copy(most, most, ssem.at[1]).wait()
        most = got.at[pl.ds(0, NDEV - 1)]
        pltpu.make_async_copy(most, most, ssem.at[0]).wait()

    vm = pl.BlockSpec(memory_space=VMEM)
    return pl.pallas_call(
        kernel, name='reduce_shares',
        out_shape=[jax.ShapeDtypeStruct((8, D), F32), jax.ShapeDtypeStruct((NDEV, RED - 8, D), F32)],
        in_specs=[vm], out_specs=[vm, vm],
        scratch_shapes=[VMEM((NDEV, RED, D), F32), VMEM((RED - 8, D), F32)] + [pltpu.SemaphoreType.DMA((2,))] * 3,
        compiler_params=pltpu.CompilerParams(collective_id=cid, has_side_effects=True))(parts)


def solution(mesh):
    def device_step(feat_cols, w_self1_rows, w_nbr1_rows, nbr_rows, mask_rows, w_self2, w_nbr2, w_self3, w_nbr3, label_rows):
        nbr_t, mask_t = nbr_rows.T, mask_rows.T
        deg = jnp.sum(mask_t, axis=0)
        deg_wide = jnp.broadcast_to(deg.astype(F32)[:, None], (R, D))
        idx = jnp.where(mask_t > 0, nbr_t, N).reshape(E)
        w1_rows = jnp.concatenate([w_self1_rows, w_nbr1_rows], axis=1)
        out_going = jnp.concatenate(
            [feat_cols.T.reshape(4, NDEV, R), jnp.broadcast_to(w1_rows[:, None, :], (4, NDEV, 2 * D))], axis=2)
        in_coming = lax.all_to_all(out_going, AX, 1, 0, tiled=True).reshape(D, R + 2 * D)
        feat = in_coming[:, :R].T
        w_self1, w_nbr1 = in_coming[:, R:R + D], in_coming[:, R + D:]
        lo, hi, lists = in_edges(nbr_t, mask_t, deg, 1)
        wide = lambda w: jnp.pad(w, ((0, 0), (0, D - C)))
        ws3, wn3 = wide(w_self3), wide(w_nbr3)
        agg_x, pre_one, act_one = hidden_layer(feat, idx, deg_wide, w_self1, w_nbr1, 'layer_one')
        agg_one, pre_two, act_two = hidden_layer(act_one, idx, deg_wide, w_self2, w_nbr2, 'layer_two')
        g_three, u_two, dws3, dwn3, loss = output_layer(
            act_two, idx, deg_wide, label_rows[:, None], ws3, wn3, 'layer_three')
        g_two, u_one, dws2, dwn2 = backward_layer(
            all_gather(u_two, 2, 'gather_rows'), lo, hi, lists, g_three, ws3, pre_two, act_one, agg_one, w_nbr2, 'back_two')
        dws1, dwn1 = backward_layer(
            all_gather(u_one, 2, 'gather_rows'), lo, hi, lists, g_two, w_self2, pre_one, feat, agg_x, None, 'back_one')
        cut = lambda v: v.reshape(NDEV, D // NDEV, D)
        last = jnp.concatenate([dws3[:, :D // 2], dwn3[:, :D // 2]], axis=1)
        parts = jnp.concatenate(
            [cut(v) for v in (dws1, dwn1, dws2, dwn2, last)] + [jnp.broadcast_to(loss[None, :4], (NDEV, 4, D))], axis=1)
        own, every = reduce_shares(parts, 7)
        whole = lambda j: every[:, j:j + 4].reshape(D, D)
        last = whole(8)
        return (every[0, 12, 0] / N, own[:4], own[4:], whole(0), whole(4), last[:, :C], last[:, D // 2:D // 2 + C])

    row = P(AX, None)
    return jax.shard_map(
        device_step, mesh=mesh,
        in_specs=(P(None, AX), row, row, row, row, P(), P(), P(), P(), P(AX)),
        out_specs=(P(), row, row, P(), P(), P(), P()),
        check_vma=False)
```

time: 5420 us -> 796 us (0.15)
  local copies, waits for them, and re-layouts: 2620 us -> 26.9 us
  waiting for transfers between devices: 1580 us -> 0.01 us
  other arithmetic: 1070 us -> 26.8 us
  Pallas kernels: 0 us -> 724 us
  matrix products: 79.1 us -> 0 us
    gather x30 -> x0, local copies, waits for them, and re-layouts: 2540 us -> none  [body(): return (running + wts_k[:, None] * table[ids_k].astype(jnp.float32), None)]
    reduce_scatter x3 -> x0, waiting for transfers between devices: 1070 us -> none  [the longest x1 362 us: upper_layers(): lax.psum_scatter(neighbour_mean_t(d_agg_one, nbr_rows, mask_f, degree, nu...]
    pallas_call x0 -> x12, Pallas kernels: none -> 724 us  [the longest x6 362 us: all_gather(): pl.pallas_call(kernel, out_shape=jax.ShapeDtypeStruct((rb * NDEV,) + v.sh...]
    scatter-add x20 -> x0, other arithmetic: 658 us -> none  [body(): return (running.at[ids_k].add(wts_k[:, None] * scaled), None)]
    all_gather x5 -> x0, waiting for transfers between devices: 401 us -> none  [the longest x1 120 us: upper_layers(): act_one_all = lax.all_gather(act_one, GROUP_AXIS, tiled=True)]
    add x30 -> x1, other arithmetic: 315 us -> 2.8 us  [in_edges(): src = (keys >> 4 & R - 1) + sender * R]
    psum x1 -> x0, waiting for transfers between devices: 112 us -> none  [upper_layers(): lax.psum(jnp.einsum('nh,nj->hj', act_one, g_two, preferred_element_type=j...]
    dot_general x16 -> x0, matrix products: 79.1 us -> none  [the longest x1 29.1 us: device_step(): jnp.dot(agg_x, w_nbr1_rows, preferred_element_type=jnp.float32)]
  transfers between devices with their start and end apart: 9 -> 1, of which waited for: 9 -> 0; matrix products, arithmetic and copies ran while one was open for 1% -> 5% of each run, Pallas kernels for 0% -> 3%
where the time goes in v1:
time: 796 us; the launch traced here: 788 us
  Pallas kernels  724 us (91%)
  local copies, waits for them, and re-layouts  26.9 us (3%)
  other arithmetic  26.8 us (3%)
    pallas_call x6, Pallas kernels, all_gather(): pl.pallas_call(kernel, out_shape=jax.ShapeDtypeStruct((rb * NDEV,) + v.sh...  362 us
    pallas_call x2, Pallas kernels, backward_layer(): pl.pallas_call(kernel, name=name, out_shape=outs, in_specs=specs, out_spe...  204 us
    pallas_call x2, Pallas kernels, hidden_layer(): pl.pallas_call(kernel, name=name, out_shape=[jax.ShapeDtypeStruct((R, D),...  88.5 us
    pallas_call x1, Pallas kernels, output_layer(): pl.pallas_call(kernel, name=name, out_shape=[jax.ShapeDtypeStruct((R, D),...  47.1 us
    pallas_call x1, Pallas kernels, reduce_shares(): pl.pallas_call(kernel, name='reduce_shares', out_shape=[jax.ShapeDtypeStr...  22.4 us
  transfers between devices with their start and end apart: 1, of which 0 were waited for; matrix products, arithmetic and copies ran while one was open for 5% of the time, Pallas kernels for 3%

profile of v1, /device:TPU:0, one launch (start us, length us, event | category | flops | bytes accessed | tf_op | source)
XLA Modules:
  0.0 787.8 jit_solution(16802117178227006452)
XLA Ops:
  1.4 2.2 pad_maximum_fusion
  3.6 7.5 all-to-all-start
  12.2 11.2 %sort.14 = (s32[20480]{0:T(1024)S(1)}, s32[20480]{0:T(1024)}) sort(s32[20480]{0:T(1024)S(1)} %reshape.105, s32[20480]{0:T(1024)S(1)} %iota.18), dimensions={0}, to_apply=%region_1.2 | sort | flops 307200 | bytes 327680 | tf_op jit(solution)/shard_map/sort | solution.py:389
  24.5 26.3 %gather_edges.1 = s32[6144,128]{1,0:T(8,128)} custom-call(s32[192,128]{1,0:T(8,128)} %pad_add_fusion.x_ref), custom_call_target="tpu_custom_call" | custom-call | tf_op jit(solution)/shard_map/gather_edges/pallas_call | solution.py:155
  50.8 3.1 slice_compare_fusion
  53.9 2.0 shift-right-arithmetic_subtract_fusion
  55.9 2.1 or_select_fusion
  60.2 1.4 copy.39.lab_ref
  61.8 1.9 copy.48
  65.0 2.8 add.60
  67.8 1.7 pad.23.src_hbm
  69.5 1.0 copy-done.1
  70.5 1.7 pad.24.dst_hbm
  72.7 1.6 pad.25.wt_hbm
  74.3 1.5 reshape.110
  76.4 1.0 copy.45
  77.5 67.6 %gather_rows.5.tab_hbm = bf16[65536,128]{1,0:T(8,128)(2,1)} custom-call(bf16[2048,128]{1,0:T(8,128)(2,1)} %bitcast.53), custom_call_target="tpu_custom_call" | custom-call | tf_op jit(solution)/shard_map/gather_rows/pallas_call | solution.py:155
  145.0 1.3 broadcast_in_dim.42.deg_ref
  146.4 44.3 %layer_one.1 = (bf16[2048,128]{1,0:T(8,128)(2,1)}, f32[2048,128]{1,0:T(8,128)}, bf16[2048,128]{1,0:T(8,128)(2,1)}) custom-call(s32[20480]{0:T(1024)} %reshape.108.idx_ref, bf16[65536,128]{1,0:T(8,128)(2,1)} %gather_rows.5.tab_hbm, bf16[2048,128]{1,0:T(8,128)(2,1)} %bitcast.54, f32[2048,128]{1,0:T(8,128)} %broadcast_in_dim.42.deg_ref, ...), custom_call_target="tpu_custom_call" | custom-call | tf_op jit(solution)/shard_map/layer_one/pallas_call | solution.py:235
  190.7 68.3 %gather_rows.6.tab_hbm = bf16[65536,128]{1,0:T(8,128)(2,1)} custom-call(bf16[2048,128]{1,0:T(8,128)(2,1)} %get-tuple-element.29.x_ref.act_ref), custom_call_target="tpu_custom_call" | custom-call | tf_op jit(solution)/shard_map/gather_rows/pallas_call | solution.py:155
  259.0 44.2 %layer_two.1 = (bf16[2048,128]{1,0:T(8,128)(2,1)}, f32[2048,128]{1,0:T(8,128)}, bf16[2048,128]{1,0:T(8,128)(2,1)}) custom-call(s32[20480]{0:T(1024)} %reshape.108.idx_ref, bf16[65536,128]{1,0:T(8,128)(2,1)} %gather_rows.6.tab_hbm, bf16[2048,128]{1,0:T(8,128)(2,1)} %get-tuple-element.29.x_ref.act_ref, f32[2048,128]{1,0:T(8,128)} %broadcast_in_dim.42.deg_ref, ...), custom_call_target="tpu_custom_call" | custom-call | tf_op jit(solution)/shard_map/layer_two/pallas_call | solution.py:235
  303.2 67.6 %gather_rows.7.tab_hbm = bf16[65536,128]{1,0:T(8,128)(2,1)} custom-call(bf16[2048,128]{1,0:T(8,128)(2,1)} %get-tuple-element.30.x_ref), custom_call_target="tpu_custom_call" | custom-call | tf_op jit(solution)/shard_map/gather_rows/pallas_call | solution.py:155
  370.8 47.1 %layer_three.1 = (bf16[2048,128]{1,0:T(8,128)(2,1)}, bf16[2048,128]{1,0:T(8,128)(2,1)}, f32[128,128]{1,0:T(8,128)}, f32[128,128]{1,0:T(8,128)}, f32[8,128]{1,0:T(8,128)}) custom-call(s32[20480]{0:T(1024)} %reshape.108.idx_ref, bf16[65536,128]{1,0:T(8,128)(2,1)} %gather_rows.7.tab_hbm, bf16[2048,128]{1,0:T(8,128)(2,1)} %get-tuple-element.30.x_ref, ...), custom_call_target="tpu_custom_call" | custom-call | tf_op jit(solution)/shard_map/layer_three/pallas_call | solution.py:274
  418.7 68.3 %gather_rows.8.tab_hbm = bf16[65536,128]{1,0:T(8,128)(2,1)} custom-call(bf16[2048,128]{1,0:T(8,128)(2,1)} %get-tuple-element.31.x_ref), custom_call_target="tpu_custom_call" | custom-call | tf_op jit(solution)/shard_map/gather_rows/pallas_call | solution.py:155
  487.0 102.0 %back_two.1 = (bf16[2048,128]{1,0:T(8,128)(2,1)}, bf16[2048,128]{1,0:T(8,128)(2,1)}, f32[128,128]{1,0:T(8,128)}, f32[128,128]{1,0:T(8,128)}) custom-call(s32[32]{0:T(128)} %bitcast.72, s32[32]{0:T(128)} %bitcast.70, s32[657408]{0:T(1024)} %pad.23.src_hbm, s32[657408]{0:T(1024)} %pad.24.dst_hbm, f32[657408]{0:T(1024)} %pad.25.wt_hbm, ...), custom_call_target="tpu_custom_call" | custom-call | tf_op jit(solution)/shard_map/back_two/pallas_call | solution.py:376
  589.0 63.9 %gather_rows.9.tab_hbm = bf16[65536,128]{1,0:T(8,128)(2,1)} custom-call(bf16[2048,128]{1,0:T(8,128)(2,1)} %get-tuple-element.35.x_ref), custom_call_target="tpu_custom_call" | custom-call | tf_op jit(solution)/shard_map/gather_rows/pallas_call | solution.py:155
  653.0 101.8 %back_one.1 = (f32[128,128]{1,0:T(8,128)}, f32[128,128]{1,0:T(8,128)}) custom-call(s32[32]{0:T(128)} %bitcast.73, s32[32]{0:T(128)} %bitcast.71, s32[657408]{0:T(1024)} %pad.23.src_hbm, s32[657408]{0:T(1024)} %pad.24.dst_hbm, f32[657408]{0:T(1024)} %pad.25.wt_hbm, bf16[65536,128]{1,0:T(8,128)(2,1)} %gather_rows.9.tab_hbm, ...), custom_call_target="tpu_custom_call" | custom-call | tf_op jit(solution)/shard_map/back_one/pallas_call | solution.py:376
  754.9 3.0 concatenate.19.p_ref
  757.9 22.4 %reduce_shares.1 = (f32[8,128]{1,0:T(8,128)}, f32[32,16,128]{2,1,0:T(8,128)}) custom-call(f32[32,24,128]{2,1,0:T(8,128)} %concatenate.19.p_ref), custom_call_target="tpu_custom_call" | custom-call | tf_op jit(solution)/shard_map/reduce_shares/pallas_call | solution.py:459
  780.3 1.2 slice.56
  781.5 1.7 fusion.4
  783.2 1.3 fusion.6
  (56 shorter events, 10.0 us)
Async XLA Ops:
  0.6 11.4 %copy-start.3 = (s32[2048,10]{0,1:T(8,128)S(1)}, s32[2048,10]{0,1:T(8,128)}, u32[]{:S(2)}) copy-start(s32[2048,10]{0,1:T(8,128)} %param.14) | copy-start | bytes 245764
  0.6 11.4 %copy-start.4 = (s32[2048,10]{0,1:T(8,128)S(1)}, s32[2048,10]{0,1:T(8,128)}, u32[]{:S(2)}) copy-start(s32[2048,10]{0,1:T(8,128)} %param.13) | copy-start | bytes 245764
  3.6 70.7 %all-to-all-start = ((bf16[4,32,2304]{2,0,1:T(4,128)(2,1)}), bf16[4,32,2304]{2,0,1:T(4,128)(2,1)}, u32[]{:S(2)}, u32[]{:S(2)}) async-start(bf16[4,32,2304]{2,0,1:T(4,128)(2,1)} %pad_maximum_fusion), calls=%async_computation | async-start | bytes 1179648 | tf_op jit(solution)/shard_map/all_to_all | solution.py:476
  50.8 3.1 copy-start
  53.9 2.0 copy-start.2
  55.9 2.1 copy-start.9
  55.9 2.3 copy-start.10
  55.9 4.3 copy-start.11
  67.8 2.7 copy-start.1
  589.0 63.9 %copy-start.7 = (f32[128,128]{1,0:T(8,128)S(1)}, f32[128,128]{1,0:T(8,128)}, u32[]{:S(2)}) copy-start(f32[128,128]{1,0:T(8,128)} %get-tuple-element.43) | copy-start | bytes 196612
  589.0 63.9 %copy-start.8 = (f32[128,128]{1,0:T(8,128)S(1)}, f32[128,128]{1,0:T(8,128)}, u32[]{:S(2)}) copy-start(f32[128,128]{1,0:T(8,128)} %get-tuple-element.44) | copy-start | bytes 196612
  653.0 101.9 %copy-start.5 = (f32[128,128]{1,0:T(8,128)S(1)}, f32[128,128]{1,0:T(8,128)}, u32[]{:S(2)}) copy-start(f32[128,128]{1,0:T(8,128)} %get-tuple-element.41) | copy-start | bytes 196612
  653.0 101.9 %copy-start.6 = (f32[128,128]{1,0:T(8,128)S(1)}, f32[128,128]{1,0:T(8,128)}, u32[]{:S(2)}) copy-start(f32[128,128]{1,0:T(8,128)} %get-tuple-element.42) | copy-start | bytes 196612

commit v2 on v1

v2 whole, which is shorter than its diff:
```python
import functools

import jax
import jax.numpy as jnp
from jax import lax
from jax.experimental import pallas as pl
from jax.experimental.pallas import tpu as pltpu
from jax.sharding import PartitionSpec as P

AX = 'g'
N = 65536
R = 2048
D = 128
K = 10
C = 40
NDEV = 32
E = R * K
CAP = 2048
NACC = 16
SLOTS = 8
TCH = 2048
TBUF = 6
MESH = pl.DeviceIdType.MESH
VMEM = pltpu.VMEM
BF = jnp.bfloat16
F32 = jnp.float32
VLIM = 62 * 1024 * 1024


def gather_blocks(arrays, chunks, order, lsem, rsem, sems):
    nq = len(chunks)
    me = lax.axis_index(AX)
    z, y, x, c = me // 8, lax.rem(me // 4, 2), lax.rem(me // 2, 2), lax.rem(me, 2)

    def dev(z_, y_, x_, c_):
        return ((z_ * 2 + y_) * 2 + x_) * 2 + c_

    d_x, d_y, d_up, d_dn, d_c = dev(z, y, 1 - x, c), dev(z, 1 - y, x, c), me + 8, me - 8, dev(z, y, x, 1 - c)
    bar = pltpu.get_barrier_semaphore()
    for d in (d_x, d_y, d_c):
        pl.semaphore_signal(bar, device_id=(d,), device_id_type=MESH)

    @pl.when(z < 3)
    def _():
        pl.semaphore_signal(bar, device_id=(d_up,), device_id_type=MESH)

    @pl.when(z > 0)
    def _():
        pl.semaphore_signal(bar, device_id=(d_dn,), device_id_type=MESH)

    pl.semaphore_wait(bar, 4 + lax.rem(z + 1, 4) // 2)
    sent = [[[0] for _ in range(4)] for _ in arrays]

    def place(q, zo, yo, xo):
        array, first, rows, _ = chunks[q]
        block, table = arrays[array]
        return table.at[pl.ds(pl.multiple_of(dev(zo, yo, xo, c) * block.shape[0] + first, 8), rows)]

    def slot(q, zo, yo, xo):
        return rsem.at[((zo * 2 + yo) * 2 + xo) * nq + q]

    def forward(q, zo, yo, xo, up, dn, to_x, to_y, src=None):
        dst = place(q, zo, yo, xo)
        src = dst if src is None else src
        ssem, csem = sems[chunks[q][0]]

        def send(d, ss, rs):
            pltpu.make_async_remote_copy(
                src_ref=src, dst_ref=dst, send_sem=ss, recv_sem=rs, device_id=(d,), device_id_type=MESH).start()

        if up is not None:
            @pl.when(up)
            def _():
                send(d_up, ssem.at[0], slot(q, zo, yo, xo))

            @pl.when(dn)
            def _():
                send(d_dn, ssem.at[1], slot(q, zo, yo, xo))
        for there, d, j in ((to_x, d_x, 2), (to_y, d_y, 3)):
            if there:
                send(d, ssem.at[j], slot(q, zo, yo, xo))
                sent[chunks[q][0]][j][0] += chunks[q][2]
        send(d_c, csem.at[0], csem.at[1])

    own = []
    for q in order[:nq]:
        array, first, rows, _ = chunks[q]
        forward(q, z, y, x, z < 3, z > 0, True, True, arrays[array][0].at[pl.ds(first, rows)])
    for j, (block, table) in enumerate(arrays):
        rb = block.shape[0]
        own.append(pltpu.make_async_copy(block, table.at[pl.ds(pl.multiple_of(me * rb, 8), rb)], lsem.at[j]))
        own[j].start()
    zr = [z, z + 1 - 2 * lax.rem(z, 2), 2 - z // 2, 3 - 3 * (z // 2)]

    for code in order[nq:]:
        kind, r, q = code // 100, code // 10 % 10, code % 10
        plane_first = chunks[q][3]
        zo, yo, xo = zr[r], 1 - y if kind >= 2 else y, 1 - x if kind % 2 else x
        here = place(q, zo, yo, xo)
        pltpu.make_async_remote_copy(
            src_ref=here, dst_ref=here, send_sem=sems[0][0].at[0], recv_sem=slot(q, zo, yo, xo),
            device_id=(d_x,), device_id_type=MESH).wait_recv()
        up = dn = None
        if kind == 0 or plane_first:
            up, dn = (z < 3, z > 0) if r == 0 else ((zo < z) & (z < 3), (zo > z) & (z > 0))
        column = kind == 0 and not plane_first
        across = not plane_first or r == 0
        forward(q, zo, yo, xo, up, dn,
                column or (kind == 2 and q % 2 == 1 and across), column or (kind == 1 and q % 2 == 0 and across))

    for j, (block, table) in enumerate(arrays):
        ssem, csem = sems[j]

        def wait_rows(n, sem, table=table):
            v = table.at[pl.ds(0, n)]
            pltpu.make_async_copy(v, v, sem).wait()

        own[j].wait()
        for k in (2, 3):
            wait_rows(sent[j][k][0], ssem.at[k])
        step = sum(rows * (4 if plane_first else 1) for array, _, rows, plane_first in chunks if array == j)
        for k in range(3):
            @pl.when(z == k)
            def _(k=k):
                wait_rows((k + 1) * step, ssem.at[0])

            @pl.when(z == 3 - k)
            def _(k=k):
                wait_rows((k + 1) * step, ssem.at[1])
        wait_rows(16 * block.shape[0], csem.at[0])
        wait_rows(16 * block.shape[0], csem.at[1])


def cut(*sizes, array=0, plane_first=0):
    return [(array, sum(sizes[:i]), n, i < plane_first) for i, n in enumerate(sizes)]


def steps(*words):
    every = [w // 1000 ** i % 1000 for w in words for i in reversed(range(8))]
    return [v for v in every if v != 999]


ROW_CHUNKS = cut(224, 224, 272, 272, 272, 272, 256, 256, plane_first=2)
ROW_ORDER = steps(
    2003006005000004001007, 14100013201206200204016, 12017027023207101116026, 25015036111032033034211,
    24035021213020115215106, 300110022037220125126205, 104225320113112316120136, 224102217130310203011124,
    301227234114235105132237, 135307313212122010236117, 31134210107123216315121, 202223131103127306321311,
    304030317233133222312232, 137221231326331226230302, 303214305330336332322333, 323337325335314327334324)
PACKED_CHUNKS = cut(112, 112, 144, 144, 128, 128, 128, 128, plane_first=2) + cut(168, array=1)
PACKED_ORDER = list(range(9)) + [
    kind * 100 + (s + step) * 10 + q for s in range(5) for q in range(9)
    for kind, step in ((0, 1), (1, 0), (2, 0), (3, -1)) if 0 <= s + step <= 3]


def all_gather(blocks, chunks, order, cid, name):
    n = len(blocks)

    def kernel(*refs):
        lsem, rsem, *sems = refs[2 * n:]
        gather_blocks(list(zip(refs[:n], refs[n:2 * n])), chunks, order, lsem, rsem, list(zip(sems[::2], sems[1::2])))

    dma = pltpu.SemaphoreType.DMA
    return pl.pallas_call(
        kernel, out_shape=[jax.ShapeDtypeStruct((v.shape[0] * NDEV,) + v.shape[1:], v.dtype) for v in blocks],
        in_specs=[pl.BlockSpec(memory_space=VMEM)] * n, out_specs=[pl.BlockSpec(memory_space=pl.ANY)] * n,
        scratch_shapes=[dma((n,)), dma((16 * len(chunks),))] + [dma((4,)), dma((2,))] * n, name=name,
        compiler_params=pltpu.CompilerParams(collective_id=cid, has_side_effects=True))(*blocks)


def gather_rows(v):
    return all_gather([v], ROW_CHUNKS, ROW_ORDER, 2, 'gather_rows')[0]


def dot(a, b):
    return jnp.dot(a, b, preferred_element_type=F32)


def dot_rows(a, b):
    return lax.dot_general(a, b, (((0,), (0,)), ((), ())), preferred_element_type=F32)


def dot_t(a, b):
    return lax.dot_general(a, b, (((1,), (1,)), ((), ())), preferred_element_type=F32)


CB = 256


def load_table(tab_hbm, tab, stg, tsem, w_ref=None, meanwhile=None):
    nb, ch = stg.shape[0], stg.shape[1] if w_ref is None else HALF
    stg = stg if w_ref is None else stg.at[:, pl.ds(0, HALF)]
    count = N // ch if w_ref is None else N // R

    def tcopy(i, s):
        return pltpu.make_async_copy(tab_hbm.at[pl.ds(pl.multiple_of(i * ch, ch), ch), :], stg.at[s], tsem.at[s])

    for s in range(nb - 1):
        tcopy(s, s).start()
    if meanwhile is not None:
        meanwhile()

    def conv(i, _):
        s = lax.rem(i, nb)
        tcopy(i, s).wait()

        @pl.when(i + nb - 1 < count)
        def _():
            tcopy(i + nb - 1, lax.rem(i + nb - 1, nb)).start()

        if w_ref is None:
            tab[pl.ds(pl.multiple_of(i * ch, ch), ch), :] = stg[s].astype(F32)
        else:
            for half in range(2):
                for q in range(HALF // CB):
                    r = pl.ds(pl.multiple_of(i * R + half * HALF + q * CB, CB), CB)
                    tab[r, :] = dot_t(stg[s, q * CB:(q + 1) * CB, :], w_ref[half]).astype(BF).astype(F32)
        return 0

    lax.fori_loop(0, count, conv, 0)


def table_mean(tab_hbm, idx_ref, tab, stg, acc, tsem):
    load_table(tab_hbm, tab, stg, tsem)
    tab[pl.ds(N, 8), :] = jnp.zeros((8, D), F32)

    def body(b, _):
        for u in range(8):
            r = b * 8 + u
            v = [tab[pl.ds(idx_ref[k * R + r], 1), :] for k in range(K)]
            while len(v) > 1:
                v = [v[j] + v[j + 1] if j + 1 < len(v) else v[j] for j in range(0, len(v), 2)]
            acc[pl.ds(r, 1), :] = v[0]
        return 0

    lax.fori_loop(0, R // 8, body, 0)


TABLE = [VMEM((N + 8, D), F32), VMEM((TBUF, TCH, D), BF), VMEM((R, D), F32), pltpu.SemaphoreType.DMA((TBUF,))]


def hidden_layer(v, idx, deg, w_self, w_nbr, name):
    def kernel(idx_ref, tab_hbm, x_ref, deg_ref, ws_ref, wn_ref, agg_ref, pre_ref, act_ref, tab, stg, acc, tsem):
        table_mean(tab_hbm, idx_ref, tab, stg, acc, tsem)

        def block(i, _):
            r = pl.ds(pl.multiple_of(i * CB, CB), CB)
            agg = (acc[r, :] / deg_ref[r, :]).astype(BF)
            agg_ref[r, :] = agg
            pre = dot(x_ref[r, :], ws_ref[...]) + dot(agg, wn_ref[...])
            pre_ref[r, :] = pre
            act_ref[r, :] = jnp.maximum(pre, 0.0).astype(BF)
            return 0

        lax.fori_loop(0, R // CB, block, 0)

    vm = pl.BlockSpec(memory_space=VMEM)
    return pl.pallas_call(
        kernel, name=name,
        out_shape=[jax.ShapeDtypeStruct((R, D), BF), jax.ShapeDtypeStruct((R, D), F32), jax.ShapeDtypeStruct((R, D), BF)],
        in_specs=[pl.BlockSpec(memory_space=pltpu.SMEM), pl.BlockSpec(memory_space=pl.ANY), vm, vm, vm, vm],
        out_specs=[vm] * 3, scratch_shapes=TABLE, compiler_params=pltpu.CompilerParams(vmem_limit_bytes=VLIM),
    )(idx, gather_rows(v), v, deg, w_self, w_nbr)


HALF = R // 2


def output_layer(v, idx, deg, labels, w_self, w_nbr, name):
    def kernel(idx_ref, tab_hbm, x_ref, deg_ref, lab_ref, ws_ref, wn_ref, g_ref, dws_ref, dwn_ref, loss_ref,
               tab, stg, acc, tsem):
        table_mean(tab_hbm, idx_ref, tab, stg, acc, tsem)
        dws_ref[...] = jnp.zeros((D, D), F32)
        dwn_ref[...] = jnp.zeros((D, D), F32)
        lane = lax.broadcasted_iota(jnp.int32, (CB, D), 1)

        def part(start, half):
            r = pl.ds(pl.multiple_of(start, CB), CB)
            act = x_ref[r, :]
            agg = (acc[r, :] / deg_ref[r, :]).astype(BF)
            logits = dot(act, ws_ref[half]) + dot(agg, wn_ref[half])
            col = lane - half * (D // 2)
            live = (col >= 0) & (col < C)
            top = jnp.max(jnp.where(live, logits, -jnp.inf), axis=1, keepdims=True)
            ex = jnp.where(live, jnp.exp(logits - top), 0.0)
            norm = top + jnp.log(jnp.sum(ex, axis=1, keepdims=True))
            hot = jnp.where(col == lab_ref[r, :], 1.0, 0.0)
            loss = jnp.sum(jnp.where(live, hot * (norm - logits), 0.0))
            prob = jnp.where(live, jnp.exp(logits - norm), 0.0)
            g = ((prob - hot) / N).astype(BF)
            dws_ref[...] += dot_rows(act, g)
            dwn_ref[...] += dot_rows(agg, g)
            return g, loss

        def block(i, loss):
            g_low, loss_low = part(i * CB, 0)
            g_high, loss_high = part(i * CB + HALF, 1)
            g_ref[pl.ds(pl.multiple_of(i * CB, CB), CB), :] = jnp.where(lane < D // 2, g_low, g_high)
            return loss + loss_low + loss_high

        loss = lax.fori_loop(0, HALF // CB, block, jnp.float32(0.0))
        loss_ref[...] = jnp.full((8, D), loss, F32)

    vm = pl.BlockSpec(memory_space=VMEM)
    return pl.pallas_call(
        kernel, name=name,
        out_shape=[jax.ShapeDtypeStruct((HALF, D), BF), jax.ShapeDtypeStruct((D, D), F32),
                   jax.ShapeDtypeStruct((D, D), F32), jax.ShapeDtypeStruct((8, D), F32)],
        in_specs=[pl.BlockSpec(memory_space=pltpu.SMEM), pl.BlockSpec(memory_space=pl.ANY)] + [vm] * 5,
        out_specs=[vm] * 4, scratch_shapes=TABLE, compiler_params=pltpu.CompilerParams(vmem_limit_bytes=VLIM),
    )(idx, gather_rows(v), v, deg, labels, w_self, w_nbr)


def table_mean_t(lo_ref, hi_ref, src_hbm, dst_hbm, wt_hbm, tab_hbm, tab, stg, accs, lists, tsem, lsem, wt_ref):
    src, dst, wt = lists

    def list_copies(s, part, slot):
        off = pl.multiple_of(s * SPAN + (lo_ref[s] // 1024) * 1024 + part * CAP, 1024)
        return [pltpu.make_async_copy(h.at[pl.ds(off, CAP)], b.at[pl.ds(pl.multiple_of(slot * CAP, CAP), CAP)], lsem.at[j, slot])
                for j, (h, b) in enumerate(((src_hbm, src), (dst_hbm, dst), (wt_hbm, wt)))]

    for s in range(SLOTS - 1):
        for cp in list_copies(s, 0, s):
            cp.start()

    def clear():
        for a in accs:
            a[...] = jnp.zeros(a.shape, F32)

    load_table(tab_hbm, tab, stg, tsem, wt_ref, clear)

    def run(slot, first, last):
        def body(b, _):
            for u in range(NACC):
                e = slot * CAP + b * NACC + u
                d = pl.ds(dst[e], 1)
                accs[u][d, :] += tab[pl.ds(src[e], 1), :] * wt[e]
            return 0

        lax.fori_loop(first // NACC, (last + NACC - 1) // NACC, body, 0)

    def sender(s, _):
        slot = lax.rem(s, SLOTS)
        for cp in list_copies(s, 0, slot):
            cp.wait()

        @pl.when(s + SLOTS - 1 < NDEV)
        def _():
            for cp in list_copies(s + SLOTS - 1, 0, lax.rem(s + SLOTS - 1, SLOTS)):
                cp.start()

        base = (lo_ref[s] // 1024) * 1024
        run(slot, lo_ref[s] - base, jnp.minimum(hi_ref[s] - base, CAP))

        def more(p, _):
            for cp in list_copies(s, p, slot):
                cp.start()
            for cp in list_copies(s, p, slot):
                cp.wait()
            run(slot, 0, jnp.minimum(hi_ref[s] - base - p * CAP, CAP))
            return 0

        lax.fori_loop(1, (hi_ref[s] - base + CAP - 1) // CAP, more, 0)
        return 0

    lax.fori_loop(0, NDEV, sender, 0)


def backward_layer(table, lo, hi, lists, g_up, w_self, pre, act, agg, w_nbr, w_up, name):
    last = w_up is None

    def kernel(lo_ref, hi_ref, src_hbm, dst_hbm, wt_hbm, tab_hbm, gu_ref, ws_ref, pre_ref, act_ref, agg_ref, *rest):
        wu_ref = None
        if last:
            dws_ref, dwn_ref = rest[:2]
            rest = rest[2:]
        else:
            wn_ref, wu_ref, g_ref, u_ref, dws_ref, dwn_ref = rest[:6]
            rest = rest[6:]
        tab, stg = rest[:2]
        accs = rest[2:2 + NACC]
        src, dst, wt, tsem, lsem = rest[2 + NACC:]
        table_mean_t(lo_ref, hi_ref, src_hbm, dst_hbm, wt_hbm, tab_hbm, tab, stg, accs, (src, dst, wt), tsem, lsem, wu_ref)
        dws_ref[...] = jnp.zeros((D, D), F32)
        dwn_ref[...] = jnp.zeros((D, D), F32)

        def part(start, up):
            r = pl.ds(pl.multiple_of(start, CB), CB)
            back = [a[r, :] for a in accs]
            while len(back) > 1:
                back = [back[j] + back[j + 1] for j in range(0, len(back), 2)]
            g = jnp.where(pre_ref[r, :] > 0, up + back[0], 0.0).astype(BF)
            dws_ref[...] += dot_rows(act_ref[r, :], g)
            dwn_ref[...] += dot_rows(agg_ref[r, :], g)
            if not last:
                g_ref[r, :] = g
                u_ref[r, :] = dot_t(g, wn_ref[...]).astype(BF)

        def block(i, _):
            if last:
                part(i * CB, dot_t(gu_ref[pl.ds(pl.multiple_of(i * CB, CB), CB), :], ws_ref[...]))
            else:
                gu = gu_ref[pl.ds(pl.multiple_of(i * CB, CB), CB), :]
                part(i * CB, dot_t(gu, ws_ref[0]))
                part(i * CB + HALF, dot_t(gu, ws_ref[1]))
            return 0

        lax.fori_loop(0, (R if last else HALF) // CB, block, 0)

    vm, sm, hb = (pl.BlockSpec(memory_space=m) for m in (VMEM, pltpu.SMEM, pl.ANY))
    outs = [jax.ShapeDtypeStruct((D, D), F32)] * 2
    args = [lo, hi, *lists, table, g_up, w_self, pre, act, agg]
    specs = [sm, sm, hb, hb, hb, hb, vm, vm, vm, vm, vm]
    if not last:
        outs = [jax.ShapeDtypeStruct((R, D), BF)] * 2 + outs
        args += [w_nbr, w_up]
        specs += [vm, vm]
    return pl.pallas_call(
        kernel, name=name, out_shape=outs, in_specs=specs, out_specs=[vm] * len(outs),
        scratch_shapes=[VMEM((N, D), F32), VMEM((TBUF, TCH, D), BF)] + [VMEM((R + 8, D), F32)] * NACC
        + [pltpu.SMEM((SLOTS * CAP,), jnp.int32), pltpu.SMEM((SLOTS * CAP,), jnp.int32), pltpu.SMEM((SLOTS * CAP,), F32),
           pltpu.SemaphoreType.DMA((TBUF,)), pltpu.SemaphoreType.DMA((3, SLOTS))],
        compiler_params=pltpu.CompilerParams(vmem_limit_bytes=VLIM))(*args)


def rank(j):
    return ((j >> 7) & (NDEV - 1)) * R + (j >> 12) * 128 + (j & 127)


SPAN = 21 * 1024


def sorted_edges(ids, live, deg):
    here = jnp.arange(R, dtype=jnp.int32)[None, :]
    key = jnp.where(live, ids * 32768 + here * 16 + deg[None, :], -1)
    key = lax.sort(key.reshape(E))
    bounds = jnp.arange(NDEV + 1, dtype=jnp.int32)
    starts = jnp.sum(((key >> 26)[None, :] < bounds[:, None]).astype(jnp.int32), axis=1)
    return jnp.concatenate([key.reshape(E // D, D), jnp.pad(starts[None, :], ((0, 7), (0, D - NDEV - 1)))])


def in_edges(every):
    me = lax.axis_index(AX)
    keys = every.reshape(NDEV, SPAN // D, D)
    sender = jnp.arange(NDEV, dtype=jnp.int32)[:, None, None]
    row = (keys >> 4) & (R - 1)
    src = rank(sender * R + row)
    dst = (keys >> 15) - me * R
    real = (dst >= 0) & (dst < R) & (keys >= 0) & (jnp.arange(SPAN // D)[None, :, None] < E // D)
    dst = jnp.where(real, dst, R)
    wt = 1.0 / jnp.maximum(keys & 15, 1).astype(F32)
    marks = keys[:, E // D, :NDEV + 1]
    lo = lax.dynamic_index_in_dim(marks, me, 1, keepdims=False)
    hi = lax.dynamic_index_in_dim(marks, me + 1, 1, keepdims=False)
    return lo, hi, (src.reshape(-1), dst.reshape(-1), wt.reshape(-1))


RED = 24


def reduce_shares(parts, cid):
    def kernel(p_ref, own_ref, all_ref, got, mine, rsem, ssem, lsem):
        me = lax.axis_index(AX)
        bar = pltpu.get_barrier_semaphore()

        def greet(k, _):
            pl.semaphore_signal(bar, device_id=(lax.rem(me + k, NDEV),), device_id_type=MESH)
            return 0

        lax.fori_loop(1, NDEV, greet, 0)
        pl.semaphore_wait(bar, NDEV - 1)

        def share(k, _):
            d = lax.rem(me + k, NDEV)
            pltpu.make_async_remote_copy(
                src_ref=p_ref.at[d], dst_ref=got.at[me], send_sem=ssem.at[0], recv_sem=rsem.at[0],
                device_id=(d,), device_id_type=MESH).start()
            return 0

        lax.fori_loop(1, NDEV, share, 0)
        own = pltpu.make_async_copy(p_ref.at[me], got.at[me], lsem.at[0])
        own.start()
        own.wait()
        most = got.at[pl.ds(0, NDEV - 1)]
        pltpu.make_async_copy(most, most, rsem.at[0]).wait()
        v = [got[d] for d in range(NDEV)]
        while len(v) > 1:
            v = [v[j] + v[j + 1] for j in range(0, len(v), 2)]
        own_ref[...] = v[0][:8]
        mine[...] = v[0][8:]

        def tell(k, _):
            d = lax.rem(me + k, NDEV)
            pltpu.make_async_remote_copy(
                src_ref=mine, dst_ref=all_ref.at[me], send_sem=ssem.at[1], recv_sem=rsem.at[1],
                device_id=(d,), device_id_type=MESH).start()
            return 0

        lax.fori_loop(1, NDEV, tell, 0)
        keep = pltpu.make_async_copy(mine, all_ref.at[me], lsem.at[1])
        keep.start()
        keep.wait()
        most = all_ref.at[pl.ds(0, NDEV - 1)]
        pltpu.make_async_copy(most, most, rsem.at[1]).wait()
        pltpu.make_async_copy(most, most, ssem.at[1]).wait()
        most = got.at[pl.ds(0, NDEV - 1)]
        pltpu.make_async_copy(most, most, ssem.at[0]).wait()

    vm = pl.BlockSpec(memory_space=VMEM)
    return pl.pallas_call(
        kernel, name='reduce_shares',
        out_shape=[jax.ShapeDtypeStruct((8, D), F32), jax.ShapeDtypeStruct((NDEV, RED - 8, D), F32)],
        in_specs=[vm], out_specs=[vm, vm],
        scratch_shapes=[VMEM((NDEV, RED, D), F32), VMEM((RED - 8, D), F32)] + [pltpu.SemaphoreType.DMA((2,))] * 3,
        compiler_params=pltpu.CompilerParams(collective_id=cid, has_side_effects=True))(parts)


def solution(mesh):
    def device_step(feat_cols, w_self1_rows, w_nbr1_rows, nbr_rows, mask_rows, w_self2, w_nbr2, w_self3, w_nbr3, label_rows):
        me = lax.axis_index(AX)
        live = mask_rows.T > 0
        ids = rank(nbr_rows.T)
        rows = jnp.concatenate([jnp.where(live, ids, N), label_rows[None, :], jnp.zeros((5, R), jnp.int32)])
        blocks = rows.reshape(16, 16, 128).transpose(1, 0, 2)
        blocks = lax.all_to_all(jnp.concatenate([blocks, blocks]), AX, 0, 0, tiled=True)
        rows = lax.dynamic_index_in_dim(blocks.reshape(16, 2, 16, 128), me // 16, 1, keepdims=False)
        rows = rows.transpose(1, 0, 2).reshape(16, R)
        idx, labels = rows[:K], rows[K]
        w1_rows = jnp.concatenate([w_self1_rows, w_nbr1_rows], axis=1)
        out_going = jnp.concatenate(
            [feat_cols.T.reshape(4, 16, NDEV, 128).transpose(2, 0, 1, 3).reshape(NDEV, 4, R),
             jnp.broadcast_to(w1_rows[None], (NDEV, 4, 2 * D))], axis=2)
        in_coming = lax.all_to_all(out_going, AX, 0, 0, tiled=True).reshape(D, R + 2 * D)
        feat = in_coming[:, :R].T
        w_self1, w_nbr1 = in_coming[:, R:R + D], in_coming[:, R + D:]
        edges = sorted_edges(ids, live, jnp.sum(mask_rows.T, axis=0))
        deg = jnp.sum((idx < N).astype(F32), axis=0)
        deg_wide = jnp.broadcast_to(deg[:, None], (R, D))
        idx = idx.reshape(E)
        halves = lambda w: jnp.stack([jnp.pad(w, ((0, 0), (0, D - C))), jnp.pad(w, ((0, 0), (D // 2, D // 2 - C)))])
        ws3, wn3 = halves(w_self3), halves(w_nbr3)
        agg_x, pre_one, act_one = hidden_layer(feat, idx, deg_wide, w_self1, w_nbr1, 'layer_one')
        agg_one, pre_two, act_two = hidden_layer(act_one, idx, deg_wide, w_self2, w_nbr2, 'layer_two')
        g_three, dws3, dwn3, loss = output_layer(act_two, idx, deg_wide, labels[:, None], ws3, wn3, 'layer_three')
        packed, edges = all_gather([g_three, edges], PACKED_CHUNKS, PACKED_ORDER, 5, 'gather_packed')
        lo, hi, lists = in_edges(edges)
        g_two, u_one, dws2, dwn2 = backward_layer(
            packed, lo, hi, lists, g_three, ws3, pre_two, act_one, agg_one, w_nbr2, wn3,
            'back_two')
        dws1, dwn1 = backward_layer(
            gather_rows(u_one), lo, hi, lists, g_two, w_self2, pre_one, feat, agg_x, None, None, 'back_one')
        cut = lambda v: v.reshape(NDEV, D // NDEV, D)
        last = jnp.concatenate([v[:, :D // 2] + v[:, D // 2:] for v in (dws3, dwn3)], axis=1)
        parts = jnp.concatenate(
            [cut(v) for v in (dws1, dwn1, dws2, dwn2, last)] + [jnp.broadcast_to(loss[None, :4], (NDEV, 4, D))], axis=1)
        own, every = reduce_shares(parts, 7)
        whole = lambda j: every[:, j:j + 4].reshape(D, D)
        last = whole(8)
        return (every[0, 12, 0] / N, own[:4], own[4:], whole(0), whole(4), last[:, :C], last[:, D // 2:D // 2 + C])

    row = P(AX, None)
    return jax.shard_map(
        device_step, mesh=mesh,
        in_specs=(P(None, AX), row, row, row, row, P(), P(), P(), P(), P(AX)),
        out_specs=(P(), row, row, P(), P(), P(), P()),
        check_vma=False)
```

time: 796 us -> 601 us (0.76)
  Pallas kernels: 724 us -> 526 us
  waiting for transfers between devices: 0.01 us -> 12.8 us
  local copies, waits for them, and re-layouts: 26.9 us -> 17.6 us
    pallas_call x2, Pallas kernels: 204 us -> 106 us  [backward_layer(): pl.pallas_call(kernel, name=name, out_shape=outs, in_specs=specs, out_spe...]
    pallas_call x7 -> x6, Pallas kernels: 409 us -> 334 us  [the longest x5 302 us: all_gather(): pl.pallas_call(kernel, out_shape=[jax.ShapeDtypeStruct((v.shape[0] * NDEV...]
    pallas_call x2, Pallas kernels: 88.5 us -> 61.9 us  [hidden_layer(): pl.pallas_call(kernel, name=name, out_shape=[jax.ShapeDtypeStruct((R, D),...]
    all_to_all x1 -> x2, waiting for transfers between devices: 0.01 us -> 12.8 us  [the longest x1 12.8 us: device_step(): lax.all_to_all(out_going, AX, 0, 0, tiled=True).reshape(D, R + 2 * D)]
  transfers between devices with their start and end apart: 1 -> 2, of which waited for: 0 -> 1; matrix products, arithmetic and copies ran while one was open for 5% -> 3% of each run, Pallas kernels for 3% -> 0%
where the time goes in v2:
time: 601 us; the launch traced here: 599 us
  Pallas kernels  526 us (88%)
  other arithmetic  27.1 us (5%)
  local copies, waits for them, and re-layouts  17.6 us (3%)
  starting transfers between devices  13.4 us (2%)
  waiting for transfers between devices  12.8 us (2%)
    pallas_call x5, Pallas kernels, all_gather(): pl.pallas_call(kernel, out_shape=[jax.ShapeDtypeStruct((v.shape[0] * NDEV...  302 us
    pallas_call x2, Pallas kernels, backward_layer(): pl.pallas_call(kernel, name=name, out_shape=outs, in_specs=specs, out_spe...  106 us
    pallas_call x2, Pallas kernels, hidden_layer(): pl.pallas_call(kernel, name=name, out_shape=[jax.ShapeDtypeStruct((R, D),...  61.9 us
    pallas_call x1, Pallas kernels, output_layer(): pl.pallas_call(kernel, name=name, out_shape=[jax.ShapeDtypeStruct((HALF,...  32.2 us
    pallas_call x1, Pallas kernels, reduce_shares(): pl.pallas_call(kernel, name='reduce_shares', out_shape=[jax.ShapeDtypeStr...  23.8 us
    all_to_all x1, waiting for transfers between devices, device_step(): lax.all_to_all(out_going, AX, 0, 0, tiled=True).reshape(D, R + 2 * D)  12.8 us
  transfers between devices with their start and end apart: 2, of which 1 were waited for; matrix products, arithmetic and copies ran while one was open for 3% of the time, Pallas kernels for 0%

profile of v2, /device:TPU:0, one launch (start us, length us, event | category | flops | bytes accessed | tf_op | source)
XLA Modules:
  0.0 599.2 jit_solution(1527901249843074303)
XLA Ops:
  0.7 1.0 reduce_sum.28
  1.7 1.0 fusion.5
  2.7 1.0 bitcast_select_fusion.1
  3.8 0.8 add_bitcast_fusion
  4.6 0.9 copy.84
  5.5 7.4 %all-to-all-start = ((s32[32,16,128]{2,1,0:T(8,128)}), s32[32,16,128]{2,1,0:T(8,128)S(1)}, u32[]{:S(2)}, u32[]{:S(2)}) async-start(s32[32,16,128]{2,1,0:T(8,128)} %copy.84), calls=%async_computation | async-start | bytes 524288 | tf_op jit(solution)/shard_map/all_to_all | solution.py:524
  13.3 11.2 %sort.14 = (s32[20480]{0:T(1024)S(1)}, s32[20480]{0:T(1024)}) sort(s32[20480]{0:T(1024)S(1)} %reshape.130, s32[20480]{0:T(1024)S(1)} %iota.23), dimensions={0}, to_apply=%region_2.3 | sort | flops 307200 | bytes 327680 | tf_op jit(solution)/shard_map/sort | solution.py:435
  25.7 1.1 pad_maximum_fusion
  26.8 6.0 %all-to-all-start.1 = ((bf16[32,4,2304]{2,1,0:T(4,128)(2,1)}), bf16[32,4,2304]{2,1,0:T(4,128)(2,1)S(1)}, u32[]{:S(2)}, u32[]{:S(2)}) async-start(bf16[32,4,2304]{2,1,0:T(4,128)(2,1)} %pad_maximum_fusion), calls=%async_computation.1 | async-start | bytes 1179648 | tf_op jit(solution)/shard_map/all_to_all | solution.py:532
  35.3 1.4 copy.92.lab_ref
  36.7 12.8 %all-to-all-done.1 = bf16[32,4,2304]{2,1,0:T(4,128)(2,1)S(1)} async-done(((bf16[32,4,2304]{2,1,0:T(4,128)(2,1)}), bf16[32,4,2304]{2,1,0:T(4,128)(2,1)S(1)}, u32[]{:S(2)}, u32[]{:S(2)}) %all-to-all-start.1) | async-done | bytes 589856 | tf_op jit(solution)/shard_map/all_to_all | solution.py:532
  50.3 1.0 copy.96
  51.3 63.0 %gather_rows.4.tab_hbm = bf16[65536,128]{1,0:T(8,128)(2,1)} custom-call(bf16[2048,128]{1,0:T(8,128)(2,1)} %bitcast.85), custom_call_target="tpu_custom_call" | custom-call | tf_op jit(solution)/shard_map/gather_rows/pallas_call | solution.py:163
  114.4 1.3 broadcast_in_dim.49.deg_ref
  115.7 31.0 %layer_one.1 = (bf16[2048,128]{1,0:T(8,128)(2,1)}, f32[2048,128]{1,0:T(8,128)}, bf16[2048,128]{1,0:T(8,128)(2,1)}) custom-call(s32[20480]{0:T(1024)} %bitcast.90, bf16[65536,128]{1,0:T(8,128)(2,1)} %gather_rows.4.tab_hbm, bf16[2048,128]{1,0:T(8,128)(2,1)} %bitcast.86, f32[2048,128]{1,0:T(8,128)} %broadcast_in_dim.49.deg_ref, ...), custom_call_target="tpu_custom_call" | custom-call | tf_op jit(solution)/shard_map/layer_one/pallas_call | solution.py:257
  146.7 63.2 %gather_rows.5.tab_hbm = bf16[65536,128]{1,0:T(8,128)(2,1)} custom-call(bf16[2048,128]{1,0:T(8,128)(2,1)} %get-tuple-element.29.refs_0_.x_ref.act_ref), custom_call_target="tpu_custom_call" | custom-call | tf_op jit(solution)/shard_map/gather_rows/pallas_call | solution.py:163
  209.9 31.0 %layer_two.1 = (bf16[2048,128]{1,0:T(8,128)(2,1)}, f32[2048,128]{1,0:T(8,128)}, bf16[2048,128]{1,0:T(8,128)(2,1)}) custom-call(s32[20480]{0:T(1024)} %bitcast.91, bf16[65536,128]{1,0:T(8,128)(2,1)} %gather_rows.5.tab_hbm, bf16[2048,128]{1,0:T(8,128)(2,1)} %get-tuple-element.29.refs_0_.x_ref.act_ref, f32[2048,128]{1,0:T(8,128)} %broadcast_in_dim.49.deg_ref, ...), custom_call_target="tpu_custom_call" | custom-call | tf_op jit(solution)/shard_map/layer_two/pallas_call | solution.py:257
  240.8 63.2 %gather_rows.6.tab_hbm = bf16[65536,128]{1,0:T(8,128)(2,1)} custom-call(bf16[2048,128]{1,0:T(8,128)(2,1)} %get-tuple-element.30.refs_0_.x_ref), custom_call_target="tpu_custom_call" | custom-call | tf_op jit(solution)/shard_map/gather_rows/pallas_call | solution.py:163
  304.0 32.2 %layer_three.1 = (bf16[1024,128]{1,0:T(8,128)(2,1)}, f32[128,128]{1,0:T(8,128)}, f32[128,128]{1,0:T(8,128)}, f32[8,128]{1,0:T(8,128)}) custom-call(s32[20480]{0:T(1024)} %bitcast.92, bf16[65536,128]{1,0:T(8,128)(2,1)} %gather_rows.6.tab_hbm, bf16[2048,128]{1,0:T(8,128)(2,1)} %get-tuple-element.30.refs_0_.x_ref, f32[2048,128]{1,0:T(8,128)} %broadcast_in_dim.49.deg_ref, ...), custom_call_target="tpu_custom_call" | custom-call | tf_op jit(solution)/shard_map/layer_three/pallas_call | solution.py:304
  336.3 49.4 %gather_packed.1 = (bf16[32768,128]{1,0:T(8,128)(2,1)}, s32[5376,128]{1,0:T(8,128)}) custom-call(bf16[1024,128]{1,0:T(8,128)(2,1)} %get-tuple-element.31.refs_0_.gu_ref, s32[168,128]{1,0:T(8,128)} %pad_add_fusion.1.refs_1_), custom_call_target="tpu_custom_call" | custom-call | tf_op jit(solution)/shard_map/gather_packed/pallas_call | solution.py:163
  385.7 3.9 divide_bitcast_fusion.wt_hbm
  391.4 4.4 bitcast_select_fusion
  395.8 53.9 %back_two.1 = (bf16[2048,128]{1,0:T(8,128)(2,1)}, bf16[2048,128]{1,0:T(8,128)(2,1)}, f32[128,128]{1,0:T(8,128)}, f32[128,128]{1,0:T(8,128)}) custom-call(s32[32]{0:T(128)} %bitcast.109, s32[32]{0:T(128)} %bitcast.111, s32[688128]{0:T(1024)} %get-tuple-element.53.src_hbm, s32[688128]{0:T(1024)} %get-tuple-element.52.dst_hbm, ...), custom_call_target="tpu_custom_call" | custom-call | tf_op jit(solution)/shard_map/back_two/pallas_call | solution.py:417
  449.8 63.3 %gather_rows.7.tab_hbm = bf16[65536,128]{1,0:T(8,128)(2,1)} custom-call(bf16[2048,128]{1,0:T(8,128)(2,1)} %get-tuple-element.37.refs_0_), custom_call_target="tpu_custom_call" | custom-call | tf_op jit(solution)/shard_map/gather_rows/pallas_call | solution.py:163
  513.3 51.7 %back_one.1 = (f32[128,128]{1,0:T(8,128)}, f32[128,128]{1,0:T(8,128)}) custom-call(s32[32]{0:T(128)} %bitcast.110, s32[32]{0:T(128)} %bitcast.112, s32[688128]{0:T(1024)} %get-tuple-element.53.src_hbm, s32[688128]{0:T(1024)} %get-tuple-element.52.dst_hbm, f32[688128]{0:T(1024)} %divide_bitcast_fusion.wt_hbm, bf16[65536,128]{1,0:T(8,128)(2,1)} %gather_rows.7.tab_hbm, ...), custom_call_target="tpu_custom_call" | custom-call | tf_op jit(solution)/shard_map/back_one/pallas_call | solution.py:417
  565.0 3.0 concatenate.34.p_ref
  568.0 23.8 %reduce_shares.1 = (f32[8,128]{1,0:T(8,128)}, f32[32,16,128]{2,1,0:T(8,128)}) custom-call(f32[32,24,128]{2,1,0:T(8,128)} %concatenate.34.p_ref), custom_call_target="tpu_custom_call" | custom-call | tf_op jit(solution)/shard_map/reduce_shares/pallas_call | solution.py:509
  591.8 1.7 fusion.7
  593.5 1.2 slice.70
  594.8 0.7 copy.100
  595.5 0.7 copy.101
  596.1 1.3 fusion.9
  (65 shorter events, 7.0 us)
Async XLA Ops:
  0.6 12.2 %copy-start.6 = (bf16[128,40]{0,1:T(8,128)(2,1)S(1)}, bf16[128,40]{0,1:T(8,128)(2,1)}, u32[]{:S(2)}) copy-start(bf16[128,40]{0,1:T(8,128)(2,1)} %param.17) | copy-start | bytes 30724
  0.6 12.4 %copy-start.7 = (bf16[128,40]{0,1:T(8,128)(2,1)S(1)}, bf16[128,40]{0,1:T(8,128)(2,1)}, u32[]{:S(2)}) copy-start(bf16[128,40]{0,1:T(8,128)(2,1)} %param.18) | copy-start | bytes 30724
  0.7 23.9 %copy-start.10 = (bf16[4,128]{1,0:T(4,128)(2,1)S(1)}, bf16[4,128]{1,0:T(4,128)(2,1)}, u32[]{:S(2)}) copy-start(bf16[4,128]{1,0:T(4,128)(2,1)} %param.11) | copy-start | bytes 3076
  0.7 23.9 %copy-start.9 = (bf16[4,128]{1,0:T(4,128)(2,1)S(1)}, bf16[4,128]{1,0:T(4,128)(2,1)}, u32[]{:S(2)}) copy-start(bf16[4,128]{1,0:T(4,128)(2,1)} %param.12) | copy-start | bytes 3076
  0.7 24.0 %copy-start.1 = (bf16[65536,4]{0,1:T(4,128)(2,1)S(1)}, bf16[65536,4]{0,1:T(4,128)(2,1)}, u32[]{:S(2)}) copy-start(bf16[65536,4]{0,1:T(4,128)(2,1)} %param.10) | copy-start | bytes 1572868
  5.5 21.3 %all-to-all-start = ((s32[32,16,128]{2,1,0:T(8,128)}), s32[32,16,128]{2,1,0:T(8,128)S(1)}, u32[]{:S(2)}, u32[]{:S(2)}) async-start(s32[32,16,128]{2,1,0:T(8,128)} %copy.84), calls=%async_computation | async-start | bytes 524288 | tf_op jit(solution)/shard_map/all_to_all | solution.py:524
  26.8 22.7 %all-to-all-start.1 = ((bf16[32,4,2304]{2,1,0:T(4,128)(2,1)}), bf16[32,4,2304]{2,1,0:T(4,128)(2,1)S(1)}, u32[]{:S(2)}, u32[]{:S(2)}) async-start(bf16[32,4,2304]{2,1,0:T(4,128)(2,1)} %pad_maximum_fusion), calls=%async_computation.1 | async-start | bytes 1179648 | tf_op jit(solution)/shard_map/all_to_all | solution.py:532
  385.6 3.9 copy-start
  449.7 63.3 %copy-start.8 = (f32[8,128]{1,0:T(8,128)S(1)}, f32[8,128]{1,0:T(8,128)}, u32[]{:S(2)}) copy-start(f32[8,128]{1,0:T(8,128)} %get-tuple-element.47) | copy-start | bytes 12292
  449.7 63.3 %copy-start.2 = (f32[128,128]{1,0:T(8,128)S(1)}, f32[128,128]{1,0:T(8,128)}, u32[]{:S(2)}) copy-start(f32[128,128]{1,0:T(8,128)} %get-tuple-element.45) | copy-start | bytes 196612
  449.8 63.3 %copy-start.3 = (f32[128,128]{1,0:T(8,128)S(1)}, f32[128,128]{1,0:T(8,128)}, u32[]{:S(2)}) copy-start(f32[128,128]{1,0:T(8,128)} %get-tuple-element.46) | copy-start | bytes 196612
  513.3 51.7 %copy-start.4 = (f32[128,128]{1,0:T(8,128)S(1)}, f32[128,128]{1,0:T(8,128)}, u32[]{:S(2)}) copy-start(f32[128,128]{1,0:T(8,128)} %get-tuple-element.43) | copy-start | bytes 196612
  513.3 51.7 %copy-start.5 = (f32[128,128]{1,0:T(8,128)S(1)}, f32[128,128]{1,0:T(8,128)}, u32[]{:S(2)}) copy-start(f32[128,128]{1,0:T(8,128)} %get-tuple-element.44) | copy-start | bytes 196612

commit v3 on v2

--- a/solution.py
+++ b/solution.py
@@ -1,11 +1,10 @@
-import functools
-
 import jax
 import jax.numpy as jnp
 from jax import lax
 from jax.experimental import pallas as pl
 from jax.experimental.pallas import tpu as pltpu
 from jax.sharding import PartitionSpec as P
+
 
 AX = 'g'
 N = 65536
@@ -17,9 +16,11 @@
 E = R * K
 CAP = 2048
 NACC = 16
+EDGES = 32
 SLOTS = 8
-TCH = 2048
-TBUF = 6
+TBUF = 10
+BBUF = 8
+UNROLL = 16
 MESH = pl.DeviceIdType.MESH
 VMEM = pltpu.VMEM
 BF = jnp.bfloat16
@@ -152,7 +153,7 @@
     for kind, step in ((0, 1), (1, 0), (2, 0), (3, -1)) if 0 <= s + step <= 3]
 
 
-def all_gather(blocks, chunks, order, cid, name):
+def all_gather(blocks, chunks, order, cid):
     n = len(blocks)
 
     def kernel(*refs):
@@ -163,12 +164,12 @@
     return pl.pallas_call(
         kernel, out_shape=[jax.ShapeDtypeStruct((v.shape[0] * NDEV,) + v.shape[1:], v.dtype) for v in blocks],
         in_specs=[pl.BlockSpec(memory_space=VMEM)] * n, out_specs=[pl.BlockSpec(memory_space=pl.ANY)] * n,
-        scratch_shapes=[dma((n,)), dma((16 * len(chunks),))] + [dma((4,)), dma((2,))] * n, name=name,
+        scratch_shapes=[dma((n,)), dma((16 * len(chunks),))] + [dma((4,)), dma((2,))] * n,
         compiler_params=pltpu.CompilerParams(collective_id=cid, has_side_effects=True))(*blocks)
 
 
 def gather_rows(v):
-    return all_gather([v], ROW_CHUNKS, ROW_ORDER, 2, 'gather_rows')[0]
+    return all_gather([v], ROW_CHUNKS, ROW_ORDER, 2)[0]
 
 
 def dot(a, b):
@@ -186,65 +187,67 @@
 CB = 256
 
 
-def load_table(tab_hbm, tab, stg, tsem, w_ref=None, meanwhile=None):
-    nb, ch = stg.shape[0], stg.shape[1] if w_ref is None else HALF
-    stg = stg if w_ref is None else stg.at[:, pl.ds(0, HALF)]
-    count = N // ch if w_ref is None else N // R
-
-    def tcopy(i, s):
-        return pltpu.make_async_copy(tab_hbm.at[pl.ds(pl.multiple_of(i * ch, ch), ch), :], stg.at[s], tsem.at[s])
-
-    for s in range(nb - 1):
-        tcopy(s, s).start()
+def load_table(sources, make, meanwhile=None):
+    slots = sources[0][1].shape[0]
+
+    def copies(i, slot):
+        for table, space, sem in sources:
+            n = space.shape[1]
+            rows = table.at[pl.ds(pl.multiple_of(i * n, n), n), :]
+            yield pltpu.make_async_copy(rows, space.at[slot], sem.at[slot])
+
+    for i in range(slots - 1):
+        for copy in copies(i, i):
+            copy.start()
     if meanwhile is not None:
         meanwhile()
 
-    def conv(i, _):
-        s = lax.rem(i, nb)
-        tcopy(i, s).wait()
-
-        @pl.when(i + nb - 1 < count)
+    def step(i, _):
+        slot = lax.rem(i, slots)
+        for copy in copies(i, slot):
+            copy.wait()
+
+        @pl.when(i + slots - 1 < NDEV)
         def _():
-            tcopy(i + nb - 1, lax.rem(i + nb - 1, nb)).start()
-
-        if w_ref is None:
-            tab[pl.ds(pl.multiple_of(i * ch, ch), ch), :] = stg[s].astype(F32)
-        else:
-            for half in range(2):
-                for q in range(HALF // CB):
-                    r = pl.ds(pl.multiple_of(i * R + half * HALF + q * CB, CB), CB)
-                    tab[r, :] = dot_t(stg[s, q * CB:(q + 1) * CB, :], w_ref[half]).astype(BF).astype(F32)
+            for copy in copies(i + slots - 1, lax.rem(i + slots - 1, slots)):
+                copy.start()
+
+        make(i, slot)
         return 0
 
-    lax.fori_loop(0, count, conv, 0)
+    lax.fori_loop(0, NDEV, step, 0)
 
 
 def table_mean(tab_hbm, idx_ref, tab, stg, acc, tsem):
-    load_table(tab_hbm, tab, stg, tsem)
+    def widen(i, slot):
+        tab[pl.ds(pl.multiple_of(i * R, R), R), :] = stg[slot].astype(F32)
+
+    load_table([(tab_hbm, stg, tsem)], widen)
     tab[pl.ds(N, 8), :] = jnp.zeros((8, D), F32)
+    slots = [idx_ref.at[pl.ds(k * R, R)] for k in range(K)]
 
     def body(b, _):
-        for u in range(8):
-            r = b * 8 + u
-            v = [tab[pl.ds(idx_ref[k * R + r], 1), :] for k in range(K)]
+        for u in range(UNROLL):
+            r = b * UNROLL + u
+            v = [tab[pl.ds(ids[r], 1), :] for ids in slots]
             while len(v) > 1:
                 v = [v[j] + v[j + 1] if j + 1 < len(v) else v[j] for j in range(0, len(v), 2)]
             acc[pl.ds(r, 1), :] = v[0]
         return 0
 
-    lax.fori_loop(0, R // 8, body, 0)
-
-
-TABLE = [VMEM((N + 8, D), F32), VMEM((TBUF, TCH, D), BF), VMEM((R, D), F32), pltpu.SemaphoreType.DMA((TBUF,))]
-
-
-def hidden_layer(v, idx, deg, w_self, w_nbr, name):
-    def kernel(idx_ref, tab_hbm, x_ref, deg_ref, ws_ref, wn_ref, agg_ref, pre_ref, act_ref, tab, stg, acc, tsem):
+    lax.fori_loop(0, R // UNROLL, body, 0)
+
+
+TABLE = [VMEM((N + 8, D), F32), VMEM((TBUF, R, D), BF), VMEM((R, D), F32), pltpu.SemaphoreType.DMA((TBUF,))]
+
+
+def hidden_layer(v, idx, side, w_self, w_nbr):
+    def kernel(idx_ref, tab_hbm, x_ref, side_ref, ws_ref, wn_ref, agg_ref, pre_ref, act_ref, tab, stg, acc, tsem):
         table_mean(tab_hbm, idx_ref, tab, stg, acc, tsem)
 
         def block(i, _):
             r = pl.ds(pl.multiple_of(i * CB, CB), CB)
-            agg = (acc[r, :] / deg_ref[r, :]).astype(BF)
+            agg = (acc[r, :] / side_ref[r, :1]).astype(BF)
             agg_ref[r, :] = agg
             pre = dot(x_ref[r, :], ws_ref[...]) + dot(agg, wn_ref[...])
             pre_ref[r, :] = pre
@@ -255,18 +258,18 @@
 
     vm = pl.BlockSpec(memory_space=VMEM)
     return pl.pallas_call(
-        kernel, name=name,
+        kernel,
         out_shape=[jax.ShapeDtypeStruct((R, D), BF), jax.ShapeDtypeStruct((R, D), F32), jax.ShapeDtypeStruct((R, D), BF)],
         in_specs=[pl.BlockSpec(memory_space=pltpu.SMEM), pl.BlockSpec(memory_space=pl.ANY), vm, vm, vm, vm],
         out_specs=[vm] * 3, scratch_shapes=TABLE, compiler_params=pltpu.CompilerParams(vmem_limit_bytes=VLIM),
-    )(idx, gather_rows(v), v, deg, w_self, w_nbr)
+    )(idx, gather_rows(v), v, side, w_self, w_nbr)
 
 
 HALF = R // 2
 
 
-def output_layer(v, idx, deg, labels, w_self, w_nbr, name):
-    def kernel(idx_ref, tab_hbm, x_ref, deg_ref, lab_ref, ws_ref, wn_ref, g_ref, dws_ref, dwn_ref, loss_ref,
+def output_layer(v, idx, side, w_self, w_nbr):
+    def kernel(idx_ref, tab_hbm, x_ref, side_ref, ws_ref, wn_ref, g_ref, dws_ref, dwn_ref, loss_ref,
                tab, stg, acc, tsem):
         table_mean(tab_hbm, idx_ref, tab, stg, acc, tsem)
         dws_ref[...] = jnp.zeros((D, D), F32)
@@ -276,19 +279,24 @@
         def part(start, half):
             r = pl.ds(pl.multiple_of(start, CB), CB)
             act = x_ref[r, :]
-            agg = (acc[r, :] / deg_ref[r, :]).astype(BF)
+            agg = (acc[r, :] / side_ref[r, :1]).astype(BF)
             logits = dot(act, ws_ref[half]) + dot(agg, wn_ref[half])
             col = lane - half * (D // 2)
             live = (col >= 0) & (col < C)
             top = jnp.max(jnp.where(live, logits, -jnp.inf), axis=1, keepdims=True)
             ex = jnp.where(live, jnp.exp(logits - top), 0.0)
             norm = top + jnp.log(jnp.sum(ex, axis=1, keepdims=True))
-            hot = jnp.where(col == lab_ref[r, :], 1.0, 0.0)
+            hot = jnp.where(col.astype(F32) == side_ref[r, 1:], 1.0, 0.0)
             loss = jnp.sum(jnp.where(live, hot * (norm - logits), 0.0))
             prob = jnp.where(live, jnp.exp(logits - norm), 0.0)
             g = ((prob - hot) / N).astype(BF)
             dws_ref[...] += dot_rows(act, g)
             dwn_ref[...] += dot_rows(agg, g)
+            rest = 1.0 / side_ref[r, :1]
+            for j in range(3):
+                most = rest.astype(BF)
+                g = jnp.where(col == C + j, most, g)
+                rest = rest - most.astype(F32)
             return g, loss
 
         def block(i, loss):
@@ -302,21 +310,19 @@
 
     vm = pl.BlockSpec(memory_space=VMEM)
     return pl.pallas_call(
-        kernel, name=name,
+        kernel,
         out_shape=[jax.ShapeDtypeStruct((HALF, D), BF), jax.ShapeDtypeStruct((D, D), F32),
                    jax.ShapeDtypeStruct((D, D), F32), jax.ShapeDtypeStruct((8, D), F32)],
-        in_specs=[pl.BlockSpec(memory_space=pltpu.SMEM), pl.BlockSpec(memory_space=pl.ANY)] + [vm] * 5,
+        in_specs=[pl.BlockSpec(memory_space=pltpu.SMEM), pl.BlockSpec(memory_space=pl.ANY)] + [vm] * 4,
         out_specs=[vm] * 4, scratch_shapes=TABLE, compiler_params=pltpu.CompilerParams(vmem_limit_bytes=VLIM),
-    )(idx, gather_rows(v), v, deg, labels, w_self, w_nbr)
-
-
-def table_mean_t(lo_ref, hi_ref, src_hbm, dst_hbm, wt_hbm, tab_hbm, tab, stg, accs, lists, tsem, lsem, wt_ref):
-    src, dst, wt = lists
-
+    )(idx, gather_rows(v), v, side, w_self, w_nbr)
+
+
+def table_mean_t(lo_ref, hi_ref, lists_hbm, lists, lsem, tab, accs, load):
     def list_copies(s, part, slot):
         off = pl.multiple_of(s * SPAN + (lo_ref[s] // 1024) * 1024 + part * CAP, 1024)
         return [pltpu.make_async_copy(h.at[pl.ds(off, CAP)], b.at[pl.ds(pl.multiple_of(slot * CAP, CAP), CAP)], lsem.at[j, slot])
-                for j, (h, b) in enumerate(((src_hbm, src), (dst_hbm, dst), (wt_hbm, wt)))]
+                for j, (h, b) in enumerate(zip(lists_hbm, lists))]
 
     for s in range(SLOTS - 1):
         for cp in list_copies(s, 0, s):
@@ -326,17 +332,18 @@
         for a in accs:
             a[...] = jnp.zeros(a.shape, F32)
 
-    load_table(tab_hbm, tab, stg, tsem, wt_ref, clear)
+    load(clear)
+    src, dst = [[v.at[pl.ds(u, SLOTS * CAP - EDGES)] for u in range(EDGES)] for v in lists]
 
     def run(slot, first, last):
         def body(b, _):
-            for u in range(NACC):
-                e = slot * CAP + b * NACC + u
-                d = pl.ds(dst[e], 1)
-                accs[u][d, :] += tab[pl.ds(src[e], 1), :] * wt[e]
-            return 0
-
-        lax.fori_loop(first // NACC, (last + NACC - 1) // NACC, body, 0)
+            e = slot * CAP + b * EDGES
+            for u in range(EDGES):
+                d = pl.ds(dst[u][e], 1)
+                accs[u % NACC][d, :] += tab[pl.ds(src[u][e], 1), :]
+            return 0
+
+        lax.fori_loop(first // EDGES, (last + EDGES - 1) // EDGES, body, 0)
 
     def sender(s, _):
         slot = lax.rem(s, SLOTS)
@@ -365,21 +372,38 @@
     lax.fori_loop(0, NDEV, sender, 0)
 
 
-def backward_layer(table, lo, hi, lists, g_up, w_self, pre, act, agg, w_nbr, w_up, name):
-    last = w_up is None
-
-    def kernel(lo_ref, hi_ref, src_hbm, dst_hbm, wt_hbm, tab_hbm, gu_ref, ws_ref, pre_ref, act_ref, agg_ref, *rest):
-        wu_ref = None
+def backward_layer(packed, table, lo, hi, lists, g_up, w_self, pre, act, agg, w_nbr, w_up):
+    last = table is not None
+
+    def kernel(lo_ref, hi_ref, src_hbm, dst_hbm, packed_hbm, gu_ref, ws_ref, pre_ref, act_ref, agg_ref, *rest):
         if last:
-            dws_ref, dwn_ref = rest[:2]
-            rest = rest[2:]
+            table_hbm, dws_ref, dwn_ref = rest[:3]
+            rest = rest[3:]
         else:
             wn_ref, wu_ref, g_ref, u_ref, dws_ref, dwn_ref = rest[:6]
             rest = rest[6:]
-        tab, stg = rest[:2]
-        accs = rest[2:2 + NACC]
-        src, dst, wt, tsem, lsem = rest[2 + NACC:]
-        table_mean_t(lo_ref, hi_ref, src_hbm, dst_hbm, wt_hbm, tab_hbm, tab, stg, accs, (src, dst, wt), tsem, lsem, wu_ref)
+        accs, rest = rest[:NACC], rest[NACC:]
+        src, dst, lsem, tab, spread, pstg, psem, *rest = rest
+
+        part_row = lax.broadcasted_iota(jnp.int32, (D, 2 * D), 0) - C
+        part_row -= jnp.where(lax.broadcasted_iota(jnp.int32, (D, 2 * D), 1) < D, 0, D // 2)
+        spread[...] = jnp.where((part_row >= 0) & (part_row < 3), 1.0, 0.0).astype(BF)
+
+        def make(i, slot):
+            for q in range(HALF // CB):
+                part = pstg[slot, q * CB:(q + 1) * CB, :]
+                scale = dot(part, spread[...])
+                if not last:
+                    v = dot(part, wu_ref[...]).astype(BF)
+                for half in range(2):
+                    at = half * HALF + q * CB
+                    lanes = slice(half * D, (half + 1) * D)
+                    term = rest[0][slot, at:at + CB, :] if last else v[:, lanes]
+                    tab[pl.ds(pl.multiple_of(i * R + at, CB), CB), :] = term.astype(F32) * scale[:, lanes]
+
+        sources = [(packed_hbm, pstg, psem)] + ([(table_hbm, *rest)] if last else [])
+        table_mean_t(lo_ref, hi_ref, (src_hbm, dst_hbm), (src, dst), lsem, tab, accs,
+                     lambda clear: load_table(sources, make, clear))
         dws_ref[...] = jnp.zeros((D, D), F32)
         dwn_ref[...] = jnp.zeros((D, D), F32)
 
@@ -408,17 +432,21 @@
 
     vm, sm, hb = (pl.BlockSpec(memory_space=m) for m in (VMEM, pltpu.SMEM, pl.ANY))
     outs = [jax.ShapeDtypeStruct((D, D), F32)] * 2
-    args = [lo, hi, *lists, table, g_up, w_self, pre, act, agg]
-    specs = [sm, sm, hb, hb, hb, hb, vm, vm, vm, vm, vm]
-    if not last:
+    args = [lo, hi, *lists, packed, g_up, w_self, pre, act, agg]
+    specs = [sm, sm, hb, hb, hb, vm, vm, vm, vm, vm]
+    stage = [VMEM((BBUF, HALF, D), BF), pltpu.SemaphoreType.DMA((BBUF,))]
+    if last:
+        args.append(table)
+        specs.append(hb)
+        stage += [VMEM((BBUF, R, D), BF), pltpu.SemaphoreType.DMA((BBUF,))]
+    else:
         outs = [jax.ShapeDtypeStruct((R, D), BF)] * 2 + outs
         args += [w_nbr, w_up]
         specs += [vm, vm]
     return pl.pallas_call(
-        kernel, name=name, out_shape=outs, in_specs=specs, out_specs=[vm] * len(outs),
-        scratch_shapes=[VMEM((N, D), F32), VMEM((TBUF, TCH, D), BF)] + [VMEM((R + 8, D), F32)] * NACC
-        + [pltpu.SMEM((SLOTS * CAP,), jnp.int32), pltpu.SMEM((SLOTS * CAP,), jnp.int32), pltpu.SMEM((SLOTS * CAP,), F32),
-           pltpu.SemaphoreType.DMA((TBUF,)), pltpu.SemaphoreType.DMA((3, SLOTS))],
+        kernel, out_shape=outs, in_specs=specs, out_specs=[vm] * len(outs),
+        scratch_shapes=[VMEM((R + 8, D), F32)] * NACC + [pltpu.SMEM((SLOTS * CAP,), jnp.int32)] * 2
+        + [pltpu.SemaphoreType.DMA((2, SLOTS)), VMEM((N, D), F32), VMEM((D, 2 * D), BF)] + stage,
         compiler_params=pltpu.CompilerParams(vmem_limit_bytes=VLIM))(*args)
 
 
@@ -429,12 +457,12 @@
 SPAN = 21 * 1024
 
 
-def sorted_edges(ids, live, deg):
+def sorted_edges(ids, live):
     here = jnp.arange(R, dtype=jnp.int32)[None, :]
-    key = jnp.where(live, ids * 32768 + here * 16 + deg[None, :], -1)
+    key = jnp.where(live, ids * R + here, -1)
     key = lax.sort(key.reshape(E))
     bounds = jnp.arange(NDEV + 1, dtype=jnp.int32)
-    starts = jnp.sum(((key >> 26)[None, :] < bounds[:, None]).astype(jnp.int32), axis=1)
+    starts = jnp.sum(((key >> 22)[None, :] < bounds[:, None]).astype(jnp.int32), axis=1)
     return jnp.concatenate([key.reshape(E // D, D), jnp.pad(starts[None, :], ((0, 7), (0, D - NDEV - 1)))])
 
 
@@ -442,23 +470,29 @@
     me = lax.axis_index(AX)
     keys = every.reshape(NDEV, SPAN // D, D)
     sender = jnp.arange(NDEV, dtype=jnp.int32)[:, None, None]
-    row = (keys >> 4) & (R - 1)
-    src = rank(sender * R + row)
-    dst = (keys >> 15) - me * R
+    src = rank(sender * R + (keys & (R - 1)))
+    dst = (keys >> 11) - me * R
     real = (dst >= 0) & (dst < R) & (keys >= 0) & (jnp.arange(SPAN // D)[None, :, None] < E // D)
     dst = jnp.where(real, dst, R)
-    wt = 1.0 / jnp.maximum(keys & 15, 1).astype(F32)
     marks = keys[:, E // D, :NDEV + 1]
     lo = lax.dynamic_index_in_dim(marks, me, 1, keepdims=False)
     hi = lax.dynamic_index_in_dim(marks, me + 1, 1, keepdims=False)
-    return lo, hi, (src.reshape(-1), dst.reshape(-1), wt.reshape(-1))
+    return lo, hi, (src.reshape(-1), dst.reshape(-1))
 
 
 RED = 24
 
 
-def reduce_shares(parts, cid):
-    def kernel(p_ref, own_ref, all_ref, got, mine, rsem, ssem, lsem):
+def reduce_shares(grads, loss, cid):
+    n = len(grads)
+    step = D // NDEV
+
+    def kernel(*refs):
+        loss_ref, own_ref, all_ref, p_ref, got, mine, rsem, ssem, lsem = refs[n:]
+        for d in range(NDEV):
+            for j in range(n):
+                p_ref[d, j * step:(j + 1) * step, :] = refs[j][d * step:(d + 1) * step, :]
+            p_ref[d, n * step:, :] = loss_ref[:step, :]
         me = lax.axis_index(AX)
         bar = pltpu.get_barrier_semaphore()
 
@@ -509,9 +543,9 @@
     return pl.pallas_call(
         kernel, name='reduce_shares',
         out_shape=[jax.ShapeDtypeStruct((8, D), F32), jax.ShapeDtypeStruct((NDEV, RED - 8, D), F32)],
-        in_specs=[vm], out_specs=[vm, vm],
-        scratch_shapes=[VMEM((NDEV, RED, D), F32), VMEM((RED - 8, D), F32)] + [pltpu.SemaphoreType.DMA((2,))] * 3,
-        compiler_params=pltpu.CompilerParams(collective_id=cid, has_side_effects=True))(parts)
+        in_specs=[vm] * (n + 1), out_specs=[vm, vm],
+        scratch_shapes=[VMEM((NDEV, RED, D), F32)] * 2 + [VMEM((RED - 8, D), F32)] + [pltpu.SemaphoreType.DMA((2,))] * 3,
+        compiler_params=pltpu.CompilerParams(collective_id=cid, has_side_effects=True))(*grads, loss)
 
 
 def solution(mesh):
@@ -519,40 +553,38 @@
         me = lax.axis_index(AX)
         live = mask_rows.T > 0
         ids = rank(nbr_rows.T)
+        w1_rows = jnp.concatenate([w_self1_rows, w_nbr1_rows], axis=1)
+        out_going = jnp.concatenate(
+            [feat_cols.T.reshape(4, 16, NDEV, 128).transpose(2, 0, 1, 3).reshape(NDEV, 4, R),
+             jnp.broadcast_to(w1_rows[None], (NDEV, 4, 2 * D))], axis=2)
+        in_coming = lax.all_to_all(out_going, AX, 0, 0, tiled=True)
+        edges = sorted_edges(ids, live)
         rows = jnp.concatenate([jnp.where(live, ids, N), label_rows[None, :], jnp.zeros((5, R), jnp.int32)])
         blocks = rows.reshape(16, 16, 128).transpose(1, 0, 2)
         blocks = lax.all_to_all(jnp.concatenate([blocks, blocks]), AX, 0, 0, tiled=True)
         rows = lax.dynamic_index_in_dim(blocks.reshape(16, 2, 16, 128), me // 16, 1, keepdims=False)
         rows = rows.transpose(1, 0, 2).reshape(16, R)
         idx, labels = rows[:K], rows[K]
-        w1_rows = jnp.concatenate([w_self1_rows, w_nbr1_rows], axis=1)
-        out_going = jnp.concatenate(
-            [feat_cols.T.reshape(4, 16, NDEV, 128).transpose(2, 0, 1, 3).reshape(NDEV, 4, R),
-             jnp.broadcast_to(w1_rows[None], (NDEV, 4, 2 * D))], axis=2)
-        in_coming = lax.all_to_all(out_going, AX, 0, 0, tiled=True).reshape(D, R + 2 * D)
+        in_coming = in_coming.reshape(D, R + 2 * D)
         feat = in_coming[:, :R].T
         w_self1, w_nbr1 = in_coming[:, R:R + D], in_coming[:, R + D:]
-        edges = sorted_edges(ids, live, jnp.sum(mask_rows.T, axis=0))
         deg = jnp.sum((idx < N).astype(F32), axis=0)
-        deg_wide = jnp.broadcast_to(deg[:, None], (R, D))
+        side = jnp.stack([deg, labels.astype(F32)], axis=1)
         idx = idx.reshape(E)
         halves = lambda w: jnp.stack([jnp.pad(w, ((0, 0), (0, D - C))), jnp.pad(w, ((0, 0), (D // 2, D // 2 - C)))])
         ws3, wn3 = halves(w_self3), halves(w_nbr3)
-        agg_x, pre_one, act_one = hidden_layer(feat, idx, deg_wide, w_self1, w_nbr1, 'layer_one')
-        agg_one, pre_two, act_two = hidden_layer(act_one, idx, deg_wide, w_self2, w_nbr2, 'layer_two')
-        g_three, dws3, dwn3, loss = output_layer(act_two, idx, deg_wide, labels[:, None], ws3, wn3, 'layer_three')
-        packed, edges = all_gather([g_three, edges], PACKED_CHUNKS, PACKED_ORDER, 5, 'gather_packed')
+        wn3_t = jnp.concatenate([wn3[0], wn3[1]]).T
+        agg_x, pre_one, act_one = hidden_layer(feat, idx, side, w_self1, w_nbr1)
+        agg_one, pre_two, act_two = hidden_layer(act_one, idx, side, w_self2, w_nbr2)
+        g_three, dws3, dwn3, loss = output_layer(act_two, idx, side, ws3, wn3)
+        packed, edges = all_gather([g_three, edges], PACKED_CHUNKS, PACKED_ORDER, 5)
         lo, hi, lists = in_edges(edges)
         g_two, u_one, dws2, dwn2 = backward_layer(
-            packed, lo, hi, lists, g_three, ws3, pre_two, act_one, agg_one, w_nbr2, wn3,
-            'back_two')
+            packed, None, lo, hi, lists, g_three, ws3, pre_two, act_one, agg_one, w_nbr2, wn3_t)
         dws1, dwn1 = backward_layer(
-            gather_rows(u_one), lo, hi, lists, g_two, w_self2, pre_one, feat, agg_x, None, None, 'back_one')
-        cut = lambda v: v.reshape(NDEV, D // NDEV, D)
+            packed, gather_rows(u_one), lo, hi, lists, g_two, w_self2, pre_one, feat, agg_x, None, None)
         last = jnp.concatenate([v[:, :D // 2] + v[:, D // 2:] for v in (dws3, dwn3)], axis=1)
-        parts = jnp.concatenate(
-            [cut(v) for v in (dws1, dwn1, dws2, dwn2, last)] + [jnp.broadcast_to(loss[None, :4], (NDEV, 4, D))], axis=1)
-        own, every = reduce_shares(parts, 7)
+        own, every = reduce_shares([dws1, dwn1, dws2, dwn2, last], loss, 7)
         whole = lambda j: every[:, j:j + 4].reshape(D, D)
         last = whole(8)
         return (every[0, 12, 0] / N, own[:4], own[4:], whole(0), whole(4), last[:, :C], last[:, D // 2:D // 2 + C])

time: 601 us -> 553 us (0.920)
  Pallas kernels: 526 us -> 485 us
    pallas_call x5, Pallas kernels: 200 us -> 160 us  [the longest x2 85.4 us: backward_layer(): pl.pallas_call(kernel, out_shape=outs, in_specs=specs, out_specs=[vm] * l...]
where the time goes in v3:
time: 553 us; the launch traced here: 552 us
  Pallas kernels  485 us (88%)
  other arithmetic  22.9 us (4%)
  local copies, waits for them, and re-layouts  14.8 us (3%)
  starting transfers between devices  13.3 us (2%)
  waiting for transfers between devices  12.5 us (2%)
    pallas_call x5, Pallas kernels, all_gather(): pl.pallas_call(kernel, out_shape=[jax.ShapeDtypeStruct((v.shape[0] * NDEV...  305 us
    pallas_call x2, Pallas kernels, backward_layer(): pl.pallas_call(kernel, out_shape=outs, in_specs=specs, out_specs=[vm] * l...  85.4 us
    pallas_call x2, Pallas kernels, hidden_layer(): pl.pallas_call(kernel, out_shape=[jax.ShapeDtypeStruct((R, D), BF), jax.S...  48.6 us
    pallas_call x1, Pallas kernels, output_layer(): pl.pallas_call(kernel, out_shape=[jax.ShapeDtypeStruct((HALF, D), BF), ja...  25.5 us
    pallas_call x1, Pallas kernels, reduce_shares(): pl.pallas_call(kernel, name='reduce_shares', out_shape=[jax.ShapeDtypeStr...  21.1 us
    all_to_all x1, waiting for transfers between devices, device_step(): in_coming = lax.all_to_all(out_going, AX, 0, 0, tiled=True)  12.5 us
    sort x1, other arithmetic, sorted_edges(): key = lax.sort(key.reshape(E))  11.2 us
  transfers between devices with their start and end apart: 2, of which 1 were waited for; matrix products, arithmetic and copies ran while one was open for 3% of the time, Pallas kernels for 0%

profile of v3, /device:TPU:0, one launch (start us, length us, event | category | flops | bytes accessed | tf_op | source)
XLA Modules:
  0.0 551.8 jit_solution(12974329271368545966)
XLA Ops:
  0.7 1.1 fusion.4
  1.9 1.0 bitcast_select_fusion.1
  2.9 0.8 add_bitcast_fusion
  3.7 0.9 copy.84
  4.6 7.3 %all-to-all-start = ((s32[32,16,128]{2,1,0:T(8,128)}), s32[32,16,128]{2,1,0:T(8,128)S(1)}, u32[]{:S(2)}, u32[]{:S(2)}) async-start(s32[32,16,128]{2,1,0:T(8,128)} %copy.84), calls=%async_computation | async-start | bytes 524288 | tf_op jit(solution)/shard_map/all_to_all | solution.py:564
  12.2 11.2 %sort.14 = (s32[20480]{0:T(1024)S(1)}, s32[20480]{0:T(1024)}) sort(s32[20480]{0:T(1024)S(1)} %reshape.107, s32[20480]{0:T(1024)S(1)} %iota.21), dimensions={0}, to_apply=%region_1.2 | sort | flops 307200 | bytes 327680 | tf_op jit(solution)/shard_map/sort | solution.py:463
  25.0 1.1 pad_maximum_fusion
  26.1 6.0 %all-to-all-start.1 = ((bf16[32,4,2304]{2,1,0:T(4,128)(2,1)}), bf16[32,4,2304]{2,1,0:T(4,128)(2,1)S(1)}, u32[]{:S(2)}, u32[]{:S(2)}) async-start(bf16[32,4,2304]{2,1,0:T(4,128)(2,1)} %pad_maximum_fusion), calls=%async_computation.1 | async-start | bytes 1179648 | tf_op jit(solution)/shard_map/all_to_all | solution.py:560
  32.1 0.7 copy.93.wn_ref
  34.2 0.7 copy.85
  34.9 1.4 copy.88.side_ref
  36.3 12.5 %all-to-all-done.1 = bf16[32,4,2304]{2,1,0:T(4,128)(2,1)S(1)} async-done(((bf16[32,4,2304]{2,1,0:T(4,128)(2,1)}), bf16[32,4,2304]{2,1,0:T(4,128)(2,1)S(1)}, u32[]{:S(2)}, u32[]{:S(2)}) %all-to-all-start.1) | async-done | bytes 589856 | tf_op jit(solution)/shard_map/all_to_all | solution.py:560
  49.5 1.0 copy.97
  50.6 63.5 %shard_map.153.tab_hbm = bf16[65536,128]{1,0:T(8,128)(2,1)} custom-call(bf16[2048,128]{1,0:T(8,128)(2,1)} %bitcast.77), custom_call_target="tpu_custom_call" | custom-call | tf_op jit(solution)/shard_map/pallas_call | solution.py:164
  114.0 24.3 %shard_map.154 = (bf16[2048,128]{1,0:T(8,128)(2,1)}, f32[2048,128]{1,0:T(8,128)}, bf16[2048,128]{1,0:T(8,128)(2,1)}) custom-call(s32[20480]{0:T(1024)} %bitcast.83, bf16[65536,128]{1,0:T(8,128)(2,1)} %shard_map.153.tab_hbm, bf16[2048,128]{1,0:T(8,128)(2,1)} %bitcast.78, f32[2048,2]{1,0:T(8,128)} %copy.88.side_ref, ...), custom_call_target="tpu_custom_call" | custom-call | tf_op jit(solution)/shard_map/pallas_call | solution.py:260
  138.3 63.9 %shard_map.155.tab_hbm = bf16[65536,128]{1,0:T(8,128)(2,1)} custom-call(bf16[2048,128]{1,0:T(8,128)(2,1)} %get-tuple-element.29.refs_0_.x_ref.act_ref), custom_call_target="tpu_custom_call" | custom-call | tf_op jit(solution)/shard_map/pallas_call | solution.py:164
  202.2 24.3 %shard_map.156 = (bf16[2048,128]{1,0:T(8,128)(2,1)}, f32[2048,128]{1,0:T(8,128)}, bf16[2048,128]{1,0:T(8,128)(2,1)}) custom-call(s32[20480]{0:T(1024)} %bitcast.84, bf16[65536,128]{1,0:T(8,128)(2,1)} %shard_map.155.tab_hbm, bf16[2048,128]{1,0:T(8,128)(2,1)} %get-tuple-element.29.refs_0_.x_ref.act_ref, f32[2048,2]{1,0:T(8,128)} %copy.88.side_ref, ...), custom_call_target="tpu_custom_call" | custom-call | tf_op jit(solution)/shard_map/pallas_call | solution.py:260
  226.5 63.7 %shard_map.157.tab_hbm = bf16[65536,128]{1,0:T(8,128)(2,1)} custom-call(bf16[2048,128]{1,0:T(8,128)(2,1)} %get-tuple-element.30.refs_0_.x_ref), custom_call_target="tpu_custom_call" | custom-call | tf_op jit(solution)/shard_map/pallas_call | solution.py:164
  290.2 25.5 %shard_map.158 = (bf16[1024,128]{1,0:T(8,128)(2,1)}, f32[128,128]{1,0:T(8,128)}, f32[128,128]{1,0:T(8,128)}, f32[8,128]{1,0:T(8,128)}) custom-call(s32[20480]{0:T(1024)} %bitcast.85, bf16[65536,128]{1,0:T(8,128)(2,1)} %shard_map.157.tab_hbm, bf16[2048,128]{1,0:T(8,128)(2,1)} %get-tuple-element.30.refs_0_.x_ref, f32[2048,2]{1,0:T(8,128)} %copy.88.side_ref, ...), custom_call_target="tpu_custom_call" | custom-call | tf_op jit(solution)/shard_map/pallas_call | solution.py:312
  315.8 50.1 %shard_map.159 = (bf16[32768,128]{1,0:T(8,128)(2,1)}, s32[5376,128]{1,0:T(8,128)}) custom-call(bf16[1024,128]{1,0:T(8,128)(2,1)} %get-tuple-element.31.refs_0_.gu_ref, s32[168,128]{1,0:T(8,128)} %pad_add_fusion.1.refs_1_), custom_call_target="tpu_custom_call" | custom-call | tf_op jit(solution)/shard_map/pallas_call | solution.py:164
  365.9 1.1 slice.79
  368.8 4.4 bitcast_select_fusion
  373.2 44.7 %shard_map.160 = (bf16[2048,128]{1,0:T(8,128)(2,1)}, bf16[2048,128]{1,0:T(8,128)(2,1)}, f32[128,128]{1,0:T(8,128)}, f32[128,128]{1,0:T(8,128)}) custom-call(s32[32]{0:T(128)} %bitcast.99, s32[32]{0:T(128)} %bitcast.97, s32[688128]{0:T(1024)} %get-tuple-element.53.src_hbm, s32[688128]{0:T(1024)} %get-tuple-element.52.dst_hbm, ...), custom_call_target="tpu_custom_call" | custom-call | tf_op jit(solution)/shard_map/pallas_call | solution.py:446
  417.9 63.8 %shard_map.161.rest_0_ = bf16[65536,128]{1,0:T(8,128)(2,1)} custom-call(bf16[2048,128]{1,0:T(8,128)(2,1)} %get-tuple-element.40.refs_0_), custom_call_target="tpu_custom_call" | custom-call | tf_op jit(solution)/shard_map/pallas_call | solution.py:164
  481.8 0.7 pad_maximum_fusion.3.refs_4_
  482.5 40.7 %shard_map.162 = (f32[128,128]{1,0:T(8,128)}, f32[128,128]{1,0:T(8,128)}) custom-call(s32[32]{0:T(128)} %bitcast.100, s32[32]{0:T(128)} %bitcast.98, s32[688128]{0:T(1024)} %get-tuple-element.53.src_hbm, s32[688128]{0:T(1024)} %get-tuple-element.52.dst_hbm, bf16[32768,128]{1,0:T(8,128)(2,1)} %get-tuple-element.34.packed_hbm, ...), custom_call_target="tpu_custom_call" | custom-call | tf_op jit(solution)/shard_map/pallas_call | solution.py:446
  523.2 21.1 %reduce_shares.1 = (f32[8,128]{1,0:T(8,128)}, f32[32,16,128]{2,1,0:T(8,128)}) custom-call(f32[128,128]{1,0:T(8,128)} %get-tuple-element.41.refs_0_, f32[128,128]{1,0:T(8,128)} %get-tuple-element.42.refs_1_, f32[128,128]{1,0:T(8,128)} %get-tuple-element.43.refs_2_, f32[128,128]{1,0:T(8,128)} %get-tuple-element.44.refs_3_, ...), custom_call_target="tpu_custom_call" | custom-call | tf_op jit(solution)/shard_map/reduce_shares/pallas_call | solution.py:543
  544.3 1.2 slice.66
  545.5 1.7 fusion.7
  547.2 1.3 fusion.10
  548.6 0.7 copy.102
  549.3 0.7 copy.101
  (54 shorter events, 6.1 us)
Async XLA Ops:
  0.6 11.3 %copy-start.5 = (bf16[128,40]{0,1:T(8,128)(2,1)S(1)}, bf16[128,40]{0,1:T(8,128)(2,1)}, u32[]{:S(2)}) copy-start(bf16[128,40]{0,1:T(8,128)(2,1)} %param.17) | copy-start | bytes 30724
  0.6 11.5 %copy-start.4 = (bf16[128,40]{0,1:T(8,128)(2,1)S(1)}, bf16[128,40]{0,1:T(8,128)(2,1)}, u32[]{:S(2)}) copy-start(bf16[128,40]{0,1:T(8,128)(2,1)} %param.18) | copy-start | bytes 30724
  0.7 22.8 %copy-start.1 = (bf16[65536,4]{0,1:T(4,128)(2,1)S(1)}, bf16[65536,4]{0,1:T(4,128)(2,1)}, u32[]{:S(2)}) copy-start(bf16[65536,4]{0,1:T(4,128)(2,1)} %param.10) | copy-start | bytes 1572868
  3.6 20.2 %copy-start.6 = (bf16[4,128]{1,0:T(4,128)(2,1)S(1)}, bf16[4,128]{1,0:T(4,128)(2,1)}, u32[]{:S(2)}) copy-start(bf16[4,128]{1,0:T(4,128)(2,1)} %param.12) | copy-start | bytes 3076
  3.7 20.2 %copy-start.7 = (bf16[4,128]{1,0:T(4,128)(2,1)S(1)}, bf16[4,128]{1,0:T(4,128)(2,1)}, u32[]{:S(2)}) copy-start(bf16[4,128]{1,0:T(4,128)(2,1)} %param.11) | copy-start | bytes 3076
  4.6 21.5 %all-to-all-start = ((s32[32,16,128]{2,1,0:T(8,128)}), s32[32,16,128]{2,1,0:T(8,128)S(1)}, u32[]{:S(2)}, u32[]{:S(2)}) async-start(s32[32,16,128]{2,1,0:T(8,128)} %copy.84), calls=%async_computation | async-start | bytes 524288 | tf_op jit(solution)/shard_map/all_to_all | solution.py:564
  26.1 22.6 %all-to-all-start.1 = ((bf16[32,4,2304]{2,1,0:T(4,128)(2,1)}), bf16[32,4,2304]{2,1,0:T(4,128)(2,1)S(1)}, u32[]{:S(2)}, u32[]{:S(2)}) async-start(bf16[32,4,2304]{2,1,0:T(4,128)(2,1)} %pad_maximum_fusion), calls=%async_computation.1 | async-start | bytes 1179648 | tf_op jit(solution)/shard_map/all_to_all | solution.py:560
  365.9 2.9 copy-start
  417.9 63.8 %copy-start.2 = (f32[128,128]{1,0:T(8,128)S(1)}, f32[128,128]{1,0:T(8,128)}, u32[]{:S(2)}) copy-start(f32[128,128]{1,0:T(8,128)} %get-tuple-element.45) | copy-start | bytes 196612
  417.9 63.8 %copy-start.3 = (f32[128,128]{1,0:T(8,128)S(1)}, f32[128,128]{1,0:T(8,128)}, u32[]{:S(2)}) copy-start(f32[128,128]{1,0:T(8,128)} %get-tuple-element.46) | copy-start | bytes 196612

commit v4 on v3

--- a/solution.py
+++ b/solution.py
@@ -26,6 +26,8 @@
 BF = jnp.bfloat16
 F32 = jnp.float32
 VLIM = 62 * 1024 * 1024
+LLIM = 46 * 1024 * 1024
+GLIM = 48 * 1024 * 1024
 
 
 def gather_blocks(arrays, chunks, order, lsem, rsem, sems):
@@ -147,13 +149,14 @@
     24035021213020115215106, 300110022037220125126205, 104225320113112316120136, 224102217130310203011124,
     301227234114235105132237, 135307313212122010236117, 31134210107123216315121, 202223131103127306321311,
     304030317233133222312232, 137221231326331226230302, 303214305330336332322333, 323337325335314327334324)
-PACKED_CHUNKS = cut(112, 112, 144, 144, 128, 128, 128, 128, plane_first=2) + cut(168, array=1)
-PACKED_ORDER = list(range(9)) + [
-    kind * 100 + (s + step) * 10 + q for s in range(5) for q in range(9)
+PACKED_CHUNKS = cut(144, 144, 128, 128, 128, 128, 112, 112, plane_first=2) + cut(88, 80, array=1)
+PACKED_TURNS = [8, 9, *range(8)]
+PACKED_ORDER = PACKED_TURNS + [
+    kind * 100 + (s + step) * 10 + q for s in range(5) for q in PACKED_TURNS
     for kind, step in ((0, 1), (1, 0), (2, 0), (3, -1)) if 0 <= s + step <= 3]
 
 
-def all_gather(blocks, chunks, order, cid):
+def all_gather(blocks, chunks, order, cid, limit):
     n = len(blocks)
 
     def kernel(*refs):
@@ -163,13 +166,14 @@
     dma = pltpu.SemaphoreType.DMA
     return pl.pallas_call(
         kernel, out_shape=[jax.ShapeDtypeStruct((v.shape[0] * NDEV,) + v.shape[1:], v.dtype) for v in blocks],
-        in_specs=[pl.BlockSpec(memory_space=VMEM)] * n, out_specs=[pl.BlockSpec(memory_space=pl.ANY)] * n,
+        in_specs=[pl.BlockSpec(memory_space=VMEM)] * n, out_specs=[pl.BlockSpec(memory_space=pltpu.HBM)] * n,
         scratch_shapes=[dma((n,)), dma((16 * len(chunks),))] + [dma((4,)), dma((2,))] * n,
-        compiler_params=pltpu.CompilerParams(collective_id=cid, has_side_effects=True))(*blocks)
+        compiler_params=pltpu.CompilerParams(
+            collective_id=cid, has_side_effects=True, vmem_limit_bytes=limit))(*blocks)
 
 
 def gather_rows(v):
-    return all_gather([v], ROW_CHUNKS, ROW_ORDER, 2)[0]
+    return all_gather([v], ROW_CHUNKS, ROW_ORDER, 2, GLIM)[0]
 
 
 def dot(a, b):
@@ -218,12 +222,22 @@
     lax.fori_loop(0, NDEV, step, 0)
 
 
-def table_mean(tab_hbm, idx_ref, tab, stg, acc, tsem):
+class Inputs:
+    def __init__(self, operands, spaces, sem):
+        self.copies = [pltpu.make_async_copy(a, b, sem.at[j]) for j, (a, b) in enumerate(zip(operands, spaces))]
+
+    def start(self):
+        for copy in self.copies:
+            copy.start()
+
+
+def table_mean(tab_hbm, inputs, idx_ref, tab, stg, acc, tsem):
     def widen(i, slot):
         tab[pl.ds(pl.multiple_of(i * R, R), R), :] = stg[slot].astype(F32)
 
-    load_table([(tab_hbm, stg, tsem)], widen)
+    load_table([(tab_hbm, stg, tsem)], widen, inputs.start)
     tab[pl.ds(N, 8), :] = jnp.zeros((8, D), F32)
+    inputs.copies[0].wait()
     slots = [idx_ref.at[pl.ds(k * R, R)] for k in range(K)]
 
     def body(b, _):
@@ -236,14 +250,20 @@
         return 0
 
     lax.fori_loop(0, R // UNROLL, body, 0)
-
-
-TABLE = [VMEM((N + 8, D), F32), VMEM((TBUF, R, D), BF), VMEM((R, D), F32), pltpu.SemaphoreType.DMA((TBUF,))]
+    for copy in inputs.copies[1:]:
+        copy.wait()
+
+
+TABLE = [VMEM((N + 8, D), F32), VMEM((TBUF, R, D), BF), VMEM((R, D), F32), pltpu.SemaphoreType.DMA((TBUF,)),
+         pltpu.SMEM((E,), jnp.int32), VMEM((R, D), BF), VMEM((R, 2), F32), pltpu.SemaphoreType.DMA((3,))]
+HBM = pl.BlockSpec(memory_space=pltpu.HBM)
 
 
 def hidden_layer(v, idx, side, w_self, w_nbr):
-    def kernel(idx_ref, tab_hbm, x_ref, side_ref, ws_ref, wn_ref, agg_ref, pre_ref, act_ref, tab, stg, acc, tsem):
-        table_mean(tab_hbm, idx_ref, tab, stg, acc, tsem)
+    def kernel(idx_hbm, tab_hbm, x_hbm, side_hbm, ws_ref, wn_ref, agg_ref, pre_ref, act_ref,
+               tab, stg, acc, tsem, idx_ref, x_ref, side_ref, sem):
+        inputs = Inputs((idx_hbm, x_hbm, side_hbm), (idx_ref, x_ref, side_ref), sem)
+        table_mean(tab_hbm, inputs, idx_ref, tab, stg, acc, tsem)
 
         def block(i, _):
             r = pl.ds(pl.multiple_of(i * CB, CB), CB)
@@ -260,8 +280,8 @@
     return pl.pallas_call(
         kernel,
         out_shape=[jax.ShapeDtypeStruct((R, D), BF), jax.ShapeDtypeStruct((R, D), F32), jax.ShapeDtypeStruct((R, D), BF)],
-        in_specs=[pl.BlockSpec(memory_space=pltpu.SMEM), pl.BlockSpec(memory_space=pl.ANY), vm, vm, vm, vm],
-        out_specs=[vm] * 3, scratch_shapes=TABLE, compiler_params=pltpu.CompilerParams(vmem_limit_bytes=VLIM),
+        in_specs=[HBM] * 4 + [vm] * 2,
+        out_specs=[vm] * 3, scratch_shapes=TABLE, compiler_params=pltpu.CompilerParams(vmem_limit_bytes=LLIM),
     )(idx, gather_rows(v), v, side, w_self, w_nbr)
 
 
@@ -269,9 +289,10 @@
 
 
 def output_layer(v, idx, side, w_self, w_nbr):
-    def kernel(idx_ref, tab_hbm, x_ref, side_ref, ws_ref, wn_ref, g_ref, dws_ref, dwn_ref, loss_ref,
-               tab, stg, acc, tsem):
-        table_mean(tab_hbm, idx_ref, tab, stg, acc, tsem)
+    def kernel(idx_hbm, tab_hbm, x_hbm, side_hbm, ws_ref, wn_ref, g_ref, dws_ref, dwn_ref, loss_ref,
+               tab, stg, acc, tsem, idx_ref, x_ref, side_ref, sem):
+        inputs = Inputs((idx_hbm, x_hbm, side_hbm), (idx_ref, x_ref, side_ref), sem)
+        table_mean(tab_hbm, inputs, idx_ref, tab, stg, acc, tsem)
         dws_ref[...] = jnp.zeros((D, D), F32)
         dwn_ref[...] = jnp.zeros((D, D), F32)
         lane = lax.broadcasted_iota(jnp.int32, (CB, D), 1)
@@ -313,14 +334,17 @@
         kernel,
         out_shape=[jax.ShapeDtypeStruct((HALF, D), BF), jax.ShapeDtypeStruct((D, D), F32),
                    jax.ShapeDtypeStruct((D, D), F32), jax.ShapeDtypeStruct((8, D), F32)],
-        in_specs=[pl.BlockSpec(memory_space=pltpu.SMEM), pl.BlockSpec(memory_space=pl.ANY)] + [vm] * 4,
-        out_specs=[vm] * 4, scratch_shapes=TABLE, compiler_params=pltpu.CompilerParams(vmem_limit_bytes=VLIM),
+        in_specs=[HBM] * 4 + [vm] * 2,
+        out_specs=[vm] * 4, scratch_shapes=TABLE, compiler_params=pltpu.CompilerParams(vmem_limit_bytes=LLIM),
     )(idx, gather_rows(v), v, side, w_self, w_nbr)
 
 
-def table_mean_t(lo_ref, hi_ref, lists_hbm, lists, lsem, tab, accs, load):
+def table_mean_t(lo_ref, hi_ref, lists_hbm, lists, lsem, tab, accs, load, inputs):
+    def base_of(s):
+        return jnp.minimum(lo_ref[s] // 1024, (SPAN - CAP) // 1024) * 1024
+
     def list_copies(s, part, slot):
-        off = pl.multiple_of(s * SPAN + (lo_ref[s] // 1024) * 1024 + part * CAP, 1024)
+        off = pl.multiple_of(s * SPAN + base_of(s) + part * CAP, 1024)
         return [pltpu.make_async_copy(h.at[pl.ds(off, CAP)], b.at[pl.ds(pl.multiple_of(slot * CAP, CAP), CAP)], lsem.at[j, slot])
                 for j, (h, b) in enumerate(zip(lists_hbm, lists))]
 
@@ -329,11 +353,12 @@
             cp.start()
 
     def clear():
+        inputs.start()
         for a in accs:
             a[...] = jnp.zeros(a.shape, F32)
 
     load(clear)
-    src, dst = [[v.at[pl.ds(u, SLOTS * CAP - EDGES)] for u in range(EDGES)] for v in lists]
+    src, dst = [[v.at[pl.ds(u, SLOTS * CAP - EDGES + 1)] for u in range(EDGES)] for v in lists]
 
     def run(slot, first, last):
         def body(b, _):
@@ -355,7 +380,7 @@
             for cp in list_copies(s + SLOTS - 1, 0, lax.rem(s + SLOTS - 1, SLOTS)):
                 cp.start()
 
-        base = (lo_ref[s] // 1024) * 1024
+        base = base_of(s)
         run(slot, lo_ref[s] - base, jnp.minimum(hi_ref[s] - base, CAP))
 
         def more(p, _):
@@ -370,12 +395,14 @@
         return 0
 
     lax.fori_loop(0, NDEV, sender, 0)
+    for copy in inputs.copies:
+        copy.wait()
 
 
 def backward_layer(packed, table, lo, hi, lists, g_up, w_self, pre, act, agg, w_nbr, w_up):
     last = table is not None
 
-    def kernel(lo_ref, hi_ref, src_hbm, dst_hbm, packed_hbm, gu_ref, ws_ref, pre_ref, act_ref, agg_ref, *rest):
+    def kernel(lo_ref, hi_ref, src_hbm, dst_hbm, packed_hbm, gu_hbm, pre_hbm, act_hbm, agg_hbm, ws_ref, *rest):
         if last:
             table_hbm, dws_ref, dwn_ref = rest[:3]
             rest = rest[3:]
@@ -383,7 +410,8 @@
             wn_ref, wu_ref, g_ref, u_ref, dws_ref, dwn_ref = rest[:6]
             rest = rest[6:]
         accs, rest = rest[:NACC], rest[NACC:]
-        src, dst, lsem, tab, spread, pstg, psem, *rest = rest
+        src, dst, lsem, tab, spread, gu_ref, pre_ref, act_ref, agg_ref, sem, pstg, psem, *rest = rest
+        inputs = Inputs((gu_hbm, pre_hbm, act_hbm, agg_hbm), (gu_ref, pre_ref, act_ref, agg_ref), sem)
 
         part_row = lax.broadcasted_iota(jnp.int32, (D, 2 * D), 0) - C
         part_row -= jnp.where(lax.broadcasted_iota(jnp.int32, (D, 2 * D), 1) < D, 0, D // 2)
@@ -403,7 +431,7 @@
 
         sources = [(packed_hbm, pstg, psem)] + ([(table_hbm, *rest)] if last else [])
         table_mean_t(lo_ref, hi_ref, (src_hbm, dst_hbm), (src, dst), lsem, tab, accs,
-                     lambda clear: load_table(sources, make, clear))
+                     lambda clear: load_table(sources, make, clear), inputs)
         dws_ref[...] = jnp.zeros((D, D), F32)
         dwn_ref[...] = jnp.zeros((D, D), F32)
 
@@ -430,14 +458,14 @@
 
         lax.fori_loop(0, (R if last else HALF) // CB, block, 0)
 
-    vm, sm, hb = (pl.BlockSpec(memory_space=m) for m in (VMEM, pltpu.SMEM, pl.ANY))
+    vm, sm = (pl.BlockSpec(memory_space=m) for m in (VMEM, pltpu.SMEM))
     outs = [jax.ShapeDtypeStruct((D, D), F32)] * 2
-    args = [lo, hi, *lists, packed, g_up, w_self, pre, act, agg]
-    specs = [sm, sm, hb, hb, hb, vm, vm, vm, vm, vm]
+    args = [lo, hi, *lists, packed, g_up, pre, act, agg, w_self]
+    specs = [sm, sm] + [HBM] * 7 + [vm]
     stage = [VMEM((BBUF, HALF, D), BF), pltpu.SemaphoreType.DMA((BBUF,))]
     if last:
         args.append(table)
-        specs.append(hb)
+        specs.append(HBM)
         stage += [VMEM((BBUF, R, D), BF), pltpu.SemaphoreType.DMA((BBUF,))]
     else:
         outs = [jax.ShapeDtypeStruct((R, D), BF)] * 2 + outs
@@ -446,7 +474,8 @@
     return pl.pallas_call(
         kernel, out_shape=outs, in_specs=specs, out_specs=[vm] * len(outs),
         scratch_shapes=[VMEM((R + 8, D), F32)] * NACC + [pltpu.SMEM((SLOTS * CAP,), jnp.int32)] * 2
-        + [pltpu.SemaphoreType.DMA((2, SLOTS)), VMEM((N, D), F32), VMEM((D, 2 * D), BF)] + stage,
+        + [pltpu.SemaphoreType.DMA((2, SLOTS)), VMEM((N, D), F32), VMEM((D, 2 * D), BF)]
+        + [VMEM(v.shape, v.dtype) for v in (g_up, pre, act, agg)] + [pltpu.SemaphoreType.DMA((4,))] + stage,
         compiler_params=pltpu.CompilerParams(vmem_limit_bytes=VLIM))(*args)
 
 
@@ -577,7 +606,7 @@
         agg_x, pre_one, act_one = hidden_layer(feat, idx, side, w_self1, w_nbr1)
         agg_one, pre_two, act_two = hidden_layer(act_one, idx, side, w_self2, w_nbr2)
         g_three, dws3, dwn3, loss = output_layer(act_two, idx, side, ws3, wn3)
-        packed, edges = all_gather([g_three, edges], PACKED_CHUNKS, PACKED_ORDER, 5)
+        packed, edges = all_gather([g_three, edges], PACKED_CHUNKS, PACKED_ORDER, 5, VLIM)
         lo, hi, lists = in_edges(edges)
         g_two, u_one, dws2, dwn2 = backward_layer(
             packed, None, lo, hi, lists, g_three, ws3, pre_two, act_one, agg_one, w_nbr2, wn3_t)

time: 553 us -> 540 us (0.976)
  Pallas kernels: 485 us -> 468 us
    pallas_call x5, Pallas kernels: 305 us -> 298 us  [all_gather(): pl.pallas_call(kernel, out_shape=[jax.ShapeDtypeStruct((v.shape[0] * NDEV...]
    pallas_call x2, Pallas kernels: 48.6 us -> 42 us  [hidden_layer(): pl.pallas_call(kernel, out_shape=[jax.ShapeDtypeStruct((R, D), BF), jax.S...]
    unnamed x24 -> x44, local copies, waits for them, and re-layouts: 3.81 us -> 9.68 us
where the time goes in v4:
time: 540 us; the launch traced here: 539 us
  Pallas kernels  468 us (87%)
  other arithmetic  22.3 us (4%)
  local copies, waits for them, and re-layouts  17.7 us (3%)
  waiting for transfers between devices  14.7 us (3%)
  starting transfers between devices  13.3 us (2%)
    pallas_call x5, Pallas kernels, all_gather(): pl.pallas_call(kernel, out_shape=[jax.ShapeDtypeStruct((v.shape[0] * NDEV...  298 us
    pallas_call x2, Pallas kernels, backward_layer(): pl.pallas_call(kernel, out_shape=outs, in_specs=specs, out_specs=[vm] * l...  84.5 us
    pallas_call x2, Pallas kernels, hidden_layer(): pl.pallas_call(kernel, out_shape=[jax.ShapeDtypeStruct((R, D), BF), jax.S...  42 us
    pallas_call x1, Pallas kernels, output_layer(): pl.pallas_call(kernel, out_shape=[jax.ShapeDtypeStruct((HALF, D), BF), ja...  22.6 us
    pallas_call x1, Pallas kernels, reduce_shares(): pl.pallas_call(kernel, name='reduce_shares', out_shape=[jax.ShapeDtypeStr...  21.1 us
    all_to_all x1, waiting for transfers between devices, device_step(): in_coming = lax.all_to_all(out_going, AX, 0, 0, tiled=True)  14.7 us
    sort x1, other arithmetic, sorted_edges(): key = lax.sort(key.reshape(E))  11.2 us
  transfers between devices with their start and end apart: 2, of which 1 were waited for; matrix products, arithmetic and copies ran while one was open for 3% of the time, Pallas kernels for 0%

profile of v4, /device:TPU:0, one launch (start us, length us, event | category | flops | bytes accessed | tf_op | source)
XLA Modules:
  0.0 539.0 jit_solution(7357031609087963822)
XLA Ops:
  0.7 1.1 fusion.4
  1.9 1.0 bitcast_select_fusion.1
  2.9 0.8 add_bitcast_fusion
  3.7 0.9 copy.84
  4.6 7.3 %all-to-all-start = ((s32[32,16,128]{2,1,0:T(8,128)}), s32[32,16,128]{2,1,0:T(8,128)S(1)}, u32[]{:S(2)}, u32[]{:S(2)}) async-start(s32[32,16,128]{2,1,0:T(8,128)} %copy.84), calls=%async_computation | async-start | bytes 524288 | tf_op jit(solution)/shard_map/all_to_all | solution.py:593
  12.2 11.2 %sort.14 = (s32[20480]{0:T(1024)S(1)}, s32[20480]{0:T(1024)}) sort(s32[20480]{0:T(1024)S(1)} %reshape.107, s32[20480]{0:T(1024)S(1)} %iota.21), dimensions={0}, to_apply=%region_1.2 | sort | flops 307200 | bytes 327680 | tf_op jit(solution)/shard_map/sort | solution.py:492
  24.4 1.1 pad_maximum_fusion
  25.5 6.0 %all-to-all-start.1 = ((bf16[32,4,2304]{2,1,0:T(4,128)(2,1)}), bf16[32,4,2304]{2,1,0:T(4,128)(2,1)S(1)}, u32[]{:S(2)}, u32[]{:S(2)}) async-start(bf16[32,4,2304]{2,1,0:T(4,128)(2,1)} %pad_maximum_fusion), calls=%async_computation.1 | async-start | bytes 1179648 | tf_op jit(solution)/shard_map/all_to_all | solution.py:589
  33.5 14.7 %all-to-all-done.1 = bf16[32,4,2304]{2,1,0:T(4,128)(2,1)S(1)} async-done(((bf16[32,4,2304]{2,1,0:T(4,128)(2,1)}), bf16[32,4,2304]{2,1,0:T(4,128)(2,1)S(1)}, u32[]{:S(2)}, u32[]{:S(2)}) %all-to-all-start.1) | async-done | bytes 589856 | tf_op jit(solution)/shard_map/all_to_all | solution.py:589
  48.7 62.5 %shard_map.153.tab_hbm = bf16[65536,128]{1,0:T(8,128)(2,1)} custom-call(bf16[2048,128]{1,0:T(8,128)(2,1)S(1)} %bitcast.76), custom_call_target="tpu_custom_call" | custom-call | tf_op jit(solution)/shard_map/pallas_call | solution.py:167
  111.1 21.0 %shard_map.154 = (bf16[2048,128]{1,0:T(8,128)(2,1)S(1)}, f32[2048,128]{1,0:T(8,128)S(1)}, bf16[2048,128]{1,0:T(8,128)(2,1)S(1)}) custom-call(s32[20480]{0:T(1024)S(1)} %bitcast.79, bf16[65536,128]{1,0:T(8,128)(2,1)} %shard_map.153.tab_hbm, bf16[2048,128]{1,0:T(8,128)(2,1)S(1)} %bitcast.77, f32[2048,2]{1,0:T(8,128)S(1)} %copy.88.side_hbm, ...), custom_call_target="tpu_custom_call" | custom-call | tf_op jit(solution)/shard_map/pallas_call | solution.py:280
  132.2 1.0 copy-done.3
  133.2 0.8 copy-done.6
  134.0 62.8 %shard_map.155.tab_hbm = bf16[65536,128]{1,0:T(8,128)(2,1)} custom-call(bf16[2048,128]{1,0:T(8,128)(2,1)S(1)} %get-tuple-element.29.refs_0_.x_hbm.act_hbm), custom_call_target="tpu_custom_call" | custom-call | tf_op jit(solution)/shard_map/pallas_call | solution.py:167
  196.8 21.0 %shard_map.156 = (bf16[2048,128]{1,0:T(8,128)(2,1)S(1)}, f32[2048,128]{1,0:T(8,128)S(1)}, bf16[2048,128]{1,0:T(8,128)(2,1)S(1)}) custom-call(s32[20480]{0:T(1024)S(1)} %bitcast.80, bf16[65536,128]{1,0:T(8,128)(2,1)} %shard_map.155.tab_hbm, bf16[2048,128]{1,0:T(8,128)(2,1)S(1)} %get-tuple-element.29.refs_0_.x_hbm.act_hbm, f32[2048,2]{1,0:T(8,128)S(1)} %copy.88.side_hbm, ...), custom_call_target="tpu_custom_call" | custom-call | tf_op jit(solution)/shard_map/pallas_call | solution.py:280
  217.9 1.0 copy-done.4
  218.8 0.8 copy-done.7
  219.6 62.6 %shard_map.157.tab_hbm = bf16[65536,128]{1,0:T(8,128)(2,1)} custom-call(bf16[2048,128]{1,0:T(8,128)(2,1)S(1)} %get-tuple-element.30.refs_0_.x_hbm), custom_call_target="tpu_custom_call" | custom-call | tf_op jit(solution)/shard_map/pallas_call | solution.py:167
  282.3 22.6 %shard_map.158 = (bf16[1024,128]{1,0:T(8,128)(2,1)S(1)}, f32[128,128]{1,0:T(8,128)S(1)}, f32[128,128]{1,0:T(8,128)S(1)}, f32[8,128]{1,0:T(8,128)S(1)}) custom-call(s32[20480]{0:T(1024)S(1)} %bitcast.81, bf16[65536,128]{1,0:T(8,128)(2,1)} %shard_map.157.tab_hbm, bf16[2048,128]{1,0:T(8,128)(2,1)S(1)} %get-tuple-element.30.refs_0_.x_hbm, ...), custom_call_target="tpu_custom_call" | custom-call | tf_op jit(solution)/shard_map/pallas_call | solution.py:333
  305.7 47.2 %shard_map.159 = (bf16[32768,128]{1,0:T(8,128)(2,1)}, s32[5376,128]{1,0:T(8,128)}) custom-call(bf16[1024,128]{1,0:T(8,128)(2,1)} %copy-done.2, s32[168,128]{1,0:T(8,128)} %pad_add_fusion.1.refs_1_), custom_call_target="tpu_custom_call" | custom-call | tf_op jit(solution)/shard_map/pallas_call | solution.py:167
  352.9 0.9 slice.79
  355.6 1.3 copy-done.12
  356.9 4.4 bitcast_select_fusion
  361.3 44.1 %shard_map.160 = (bf16[2048,128]{1,0:T(8,128)(2,1)}, bf16[2048,128]{1,0:T(8,128)(2,1)}, f32[128,128]{1,0:T(8,128)}, f32[128,128]{1,0:T(8,128)}) custom-call(s32[32]{0:T(128)} %bitcast.99, s32[32]{0:T(128)} %bitcast.97, s32[688128]{0:T(1024)} %get-tuple-element.53.src_hbm, s32[688128]{0:T(1024)} %get-tuple-element.52.dst_hbm, ...), custom_call_target="tpu_custom_call" | custom-call | tf_op jit(solution)/shard_map/pallas_call | solution.py:474
  405.4 1.0 copy-done.8
  406.4 62.7 %shard_map.161.rest_0_ = bf16[65536,128]{1,0:T(8,128)(2,1)} custom-call(bf16[2048,128]{1,0:T(8,128)(2,1)S(1)} %copy-done.8), custom_call_target="tpu_custom_call" | custom-call | tf_op jit(solution)/shard_map/pallas_call | solution.py:167
  469.3 0.7 pad_maximum_fusion.3.refs_4_
  470.0 40.4 %shard_map.162 = (f32[128,128]{1,0:T(8,128)}, f32[128,128]{1,0:T(8,128)}) custom-call(s32[32]{0:T(128)} %bitcast.100, s32[32]{0:T(128)} %bitcast.98, s32[688128]{0:T(1024)} %get-tuple-element.53.src_hbm, s32[688128]{0:T(1024)} %get-tuple-element.52.dst_hbm, bf16[32768,128]{1,0:T(8,128)(2,1)} %get-tuple-element.34.packed_hbm, ...), custom_call_target="tpu_custom_call" | custom-call | tf_op jit(solution)/shard_map/pallas_call | solution.py:474
  510.4 21.1 %reduce_shares.1 = (f32[8,128]{1,0:T(8,128)}, f32[32,16,128]{2,1,0:T(8,128)}) custom-call(f32[128,128]{1,0:T(8,128)} %get-tuple-element.41.refs_0_, f32[128,128]{1,0:T(8,128)} %get-tuple-element.42.refs_1_, f32[128,128]{1,0:T(8,128)} %get-tuple-element.43.refs_2_, f32[128,128]{1,0:T(8,128)} %get-tuple-element.44.refs_3_, ...), custom_call_target="tpu_custom_call" | custom-call | tf_op jit(solution)/shard_map/reduce_shares/pallas_call | solution.py:572
  531.5 1.2 slice.66
  532.7 1.7 fusion.7
  534.4 1.3 fusion.10
  (74 shorter events, 7.7 us)
Async XLA Ops:
  0.6 11.3 %copy-start.15 = (bf16[128,40]{0,1:T(8,128)(2,1)S(1)}, bf16[128,40]{0,1:T(8,128)(2,1)}, u32[]{:S(2)}) copy-start(bf16[128,40]{0,1:T(8,128)(2,1)} %param.17) | copy-start | bytes 30724
  0.6 11.5 %copy-start.14 = (bf16[128,40]{0,1:T(8,128)(2,1)S(1)}, bf16[128,40]{0,1:T(8,128)(2,1)}, u32[]{:S(2)}) copy-start(bf16[128,40]{0,1:T(8,128)(2,1)} %param.18) | copy-start | bytes 30724
  0.7 22.8 %copy-start.13 = (bf16[65536,4]{0,1:T(4,128)(2,1)S(1)}, bf16[65536,4]{0,1:T(4,128)(2,1)}, u32[]{:S(2)}) copy-start(bf16[65536,4]{0,1:T(4,128)(2,1)} %param.10) | copy-start | bytes 1572868
  3.6 20.2 %copy-start.16 = (bf16[4,128]{1,0:T(4,128)(2,1)S(1)}, bf16[4,128]{1,0:T(4,128)(2,1)}, u32[]{:S(2)}) copy-start(bf16[4,128]{1,0:T(4,128)(2,1)} %param.12) | copy-start | bytes 3076
  3.7 20.2 %copy-start.17 = (bf16[4,128]{1,0:T(4,128)(2,1)S(1)}, bf16[4,128]{1,0:T(4,128)(2,1)}, u32[]{:S(2)}) copy-start(bf16[4,128]{1,0:T(4,128)(2,1)} %param.11) | copy-start | bytes 3076
  4.6 21.0 %all-to-all-start = ((s32[32,16,128]{2,1,0:T(8,128)}), s32[32,16,128]{2,1,0:T(8,128)S(1)}, u32[]{:S(2)}, u32[]{:S(2)}) async-start(s32[32,16,128]{2,1,0:T(8,128)} %copy.84), calls=%async_computation | async-start | bytes 524288 | tf_op jit(solution)/shard_map/all_to_all | solution.py:593
  23.9 258.4 %copy-start.5 = (bf16[2,128,128]{2,1,0:T(8,128)(2,1)}, bf16[2,128,128]{2,1,0:T(8,128)(2,1)S(1)}, u32[]{:S(2)}) copy-start(bf16[2,128,128]{2,1,0:T(8,128)(2,1)S(1)} %pad_maximum_fusion.1.ws_ref) | copy-start | bytes 196612
  25.5 22.6 %all-to-all-start.1 = ((bf16[32,4,2304]{2,1,0:T(4,128)(2,1)}), bf16[32,4,2304]{2,1,0:T(4,128)(2,1)S(1)}, u32[]{:S(2)}, u32[]{:S(2)}) async-start(bf16[32,4,2304]{2,1,0:T(4,128)(2,1)} %pad_maximum_fusion), calls=%async_computation.1 | async-start | bytes 1179648 | tf_op jit(solution)/shard_map/all_to_all | solution.py:589
  48.7 62.5 %copy-start = (bf16[128,2048]{0,1:T(8,128)(2,1)}, bf16[128,2048]{0,1:T(8,128)(2,1)S(1)}, u32[]{:S(2)}) copy-start(bf16[128,2048]{0,1:T(8,128)(2,1)S(1)} %copy.97) | copy-start | bytes 1572868
  132.2 1.0 copy-start.3
  133.2 0.8 copy-start.6
  134.0 62.8 %copy-start.1 = (bf16[2048,128]{1,0:T(8,128)(2,1)}, bf16[2048,128]{1,0:T(8,128)(2,1)S(1)}, u32[]{:S(2)}) copy-start(bf16[2048,128]{1,0:T(8,128)(2,1)S(1)} %get-tuple-element.29.refs_0_.x_hbm.act_hbm) | copy-start | bytes 1572868
  134.0 62.8 %copy-start.9 = (bf16[128,128]{1,0:T(8,128)(2,1)S(1)}, bf16[128,128]{1,0:T(8,128)(2,1)}, u32[]{:S(2)}) copy-start(bf16[128,128]{1,0:T(8,128)(2,1)} %rest_0_.1) | copy-start | bytes 98308
  134.0 62.8 %copy-start.10 = (bf16[128,128]{1,0:T(8,128)(2,1)S(1)}, bf16[128,128]{1,0:T(8,128)(2,1)}, u32[]{:S(2)}) copy-start(bf16[128,128]{1,0:T(8,128)(2,1)} %ws_ref.3) | copy-start | bytes 98308
  217.9 1.0 copy-start.4
  218.8 0.8 copy-start.7
  305.0 0.7 copy-start.2
  305.7 55.7 %copy-start.11 = (f32[8,128]{1,0:T(8,128)}, f32[8,128]{1,0:T(8,128)S(1)}, u32[]{:S(2)}) copy-start(f32[8,128]{1,0:T(8,128)S(1)} %get-tuple-element.47.refs_5_) | copy-start | bytes 12292
  355.1 1.8 copy-start.12
  405.4 1.0 copy-start.8
